TPU v7x, 32 devices: a whole 2x2x4 slice. The times are simulated.
32 devices in a mesh: dp: 16 (over z, y, x), tensor: 2 (over core).
Axes of the slice: x: 2, y: 2, z: 4, core: 2. Of those that a mesh axis runs over, the one named last changes fastest.
Arguments:
- inputs: bfloat16 [32, 1024, 768], P(('dp', 'tensor')), may hold values from -6 to 6
- segment_ids: int32 [32, 1024], P('dp'), may hold values from 0 to 3, never falling along the last dimension, each value on 1 to 512 neighbouring positions
- cotangent: bfloat16 [32, 1024, 768], P(('dp', 'tensor')), may hold values from -6 to 6
- attn_norm_gain: float32 [768], replicated, may hold values from 0.5 to 1.5
- attn_norm_bias: float32 [768], replicated, may hold values from -1.75 to 1.75
- qkv_weight: bfloat16 [3, 768, 768], P(None, None, 'tensor'), may hold values from -0.21875 to 0.21875
- qkv_bias: float32 [3, 768], P(None, 'tensor'), may hold values from -1.75 to 1.75
- attn_sub_gain: float32 [768], P('tensor'), may hold values from 0.5 to 1.5
- attn_sub_bias: float32 [768], P('tensor'), may hold values from -1.75 to 1.75
- out_weight: bfloat16 [768, 768], P('tensor'), may hold values from -0.21875 to 0.21875
- out_bias: float32 [768], replicated, may hold values from -1.75 to 1.75
- ffn_norm_gain: float32 [768], replicated, may hold values from 0.5 to 1.5
- ffn_norm_bias: float32 [768], replicated, may hold values from -1.75 to 1.75
- up_weight: bfloat16 [768, 3072], P(None, 'tensor'), may hold values from -0.21875 to 0.21875
- up_bias: float32 [3072], P('tensor'), may hold values from -1.75 to 1.75
- ffn_sub_gain: float32 [3072], P('tensor'), may hold values from 0.5 to 1.5
- ffn_sub_bias: float32 [3072], P('tensor'), may hold values from -1.75 to 1.75
- down_weight: bfloat16 [3072, 768], P('tensor'), may hold values from -0.109375 to 0.109375
- down_bias: float32 [768], replicated, may hold values from -1.75 to 1.75
Outputs:
- outputs: bfloat16 [32, 1024, 768], P(('dp', 'tensor'))
- input_grad: float32 [32, 1024, 768], P(('dp', 'tensor'))
- attn_norm_gain_grad: float32 [768], replicated
- attn_norm_bias_grad: float32 [768], replicated
- qkv_weight_grad: float32 [3, 768, 768], P(None, None, 'tensor')
- qkv_bias_grad: float32 [3, 768], P(None, 'tensor')
- attn_sub_gain_grad: float32 [768], P('tensor')
- attn_sub_bias_grad: float32 [768], P('tensor')
- out_weight_grad: float32 [768, 768], P('tensor')
- out_bias_grad: float32 [768], replicated
- ffn_norm_gain_grad: float32 [768], replicated
- ffn_norm_bias_grad: float32 [768], replicated
- up_weight_grad: float32 [768, 3072], P(None, 'tensor')
- up_bias_grad: float32 [3072], P('tensor')
- ffn_sub_gain_grad: float32 [3072], P('tensor')
- ffn_sub_bias_grad: float32 [3072], P('tensor')
- down_weight_grad: float32 [3072, 768], P('tensor')
- down_bias_grad: float32 [768], replicated
Inputs may be any that keep to these rules, and one draw needn't show every extreme that they name: `segment_ids`: in each row the ids never fall, so each segment is contiguous; a segment holds 1 to 512 tokens, and some segment holds exactly 512.
All inputs are finite; a program needn't handle non-finite values.
Results may differ from a plain program's by a relative error of at most 0.012.
Values may be sent and summed in bfloat16 or wider, within the bound.
A program may use at most 192 MiB of HBM per device.

v0:
```python
import math

import jax
import jax.numpy as jnp
from jax import lax
from jax.sharding import PartitionSpec as P

HD = 64
FF = 3072
BLOCK = 512


def positions(segment):
    length = segment.shape[-1]
    row_place = jnp.broadcast_to(jnp.arange(length, dtype=jnp.int32), segment.shape)
    before = jnp.concatenate([segment[..., :1] - 1, segment[..., :-1]], axis=-1)
    starts_at = jnp.where(segment != before, row_place, jnp.zeros_like(row_place))
    return row_place - lax.cummax(starts_at, axis=segment.ndim - 1)


def angles(token_place, head_size):
    half_size = head_size // 2
    frequency = jnp.exp(
        jnp.arange(half_size).astype(jnp.float32) * (-2.0 * math.log(10000.0) / head_size)
    )
    angle_rows = token_place.astype(jnp.float32)[..., None] * frequency
    return (jnp.cos(angle_rows)[..., None, :], jnp.sin(angle_rows)[..., None, :])


def rotate(values, token_place):
    half_size = values.shape[-1] // 2
    cosine, sine_part = angles(token_place, values.shape[-1])
    first_half = values[..., :half_size]
    second = values[..., half_size:]
    return jnp.concatenate(
        [first_half * cosine - second * sine_part, second * cosine + first_half * sine_part],
        axis=-1,
    )


def unrotate(gradient, token_place):
    half_size = gradient.shape[-1] // 2
    cosine, sine_part = angles(token_place, gradient.shape[-1])
    first_half = gradient[..., :half_size]
    second = gradient[..., half_size:]
    return jnp.concatenate(
        [first_half * cosine + second * sine_part, second * cosine - first_half * sine_part],
        axis=-1,
    )


def norm_rows(values, norm_gain, norm_bias):
    center = jnp.mean(values, axis=-1, keepdims=True)
    spread = jnp.mean(values * values, axis=-1, keepdims=True) - center * center
    inv_spread = lax.rsqrt(spread + 1e-05)
    unit_rows = (values - center) * inv_spread
    return (unit_rows, inv_spread, unit_rows * norm_gain + norm_bias)


def norm_back(gradient, unit_rows, inv_spread, norm_gain):
    scaled_grad = gradient * norm_gain
    return inv_spread * (
        scaled_grad
        - jnp.mean(scaled_grad, axis=-1, keepdims=True)
        - unit_rows * jnp.mean(scaled_grad * unit_rows, axis=-1, keepdims=True)
    )


def shared_norm(row_sums, values, total_width):
    center = row_sums[0][:, None] / total_width
    spread = row_sums[1][:, None] / total_width - center * center
    inv_spread = lax.rsqrt(spread + 1e-05)
    return ((values - center) * inv_spread, inv_spread)


def shared_back(row_sums, scaled_grad, unit_rows, inv_spread, total_width):
    return inv_spread * (
        scaled_grad
        - row_sums[0][:, None] / total_width
        - unit_rows * (row_sums[1][:, None] / total_width)
    )


def exact_gelu(values):
    return jax.nn.gelu(values, approximate=False)


def block_scores(query_block, key_rows, segment, first_row, key_place, score_scale):
    block_rows = query_block.shape[0]
    query_place = first_row + jnp.arange(block_rows, dtype=jnp.int32)
    query_segment = lax.dynamic_slice_in_dim(segment, first_row, block_rows, 0)
    allowed = (query_segment[:, None] == segment[None, :]) & (
        query_place[:, None] >= key_place[None, :]
    )
    scores = (
        jnp.einsum("qhd,khd->hqk", query_block, key_rows, preferred_element_type=jnp.float32)
        * score_scale
    )
    return jnp.where(allowed[None], scores, -1e30)


def attend_forward(queries, key_rows, value_rows, segment, score_scale):
    length, heads_here, head_size = queries.shape
    block_count = length // BLOCK
    key_place = jnp.arange(length, dtype=jnp.int32)

    def one_block(first_row):
        query_block = lax.dynamic_slice_in_dim(queries, first_row, BLOCK, 0)
        scores = block_scores(query_block, key_rows, segment, first_row, key_place, score_scale)
        row_peak = jnp.max(scores, axis=-1, keepdims=True)
        exp_scores = jnp.exp(scores - row_peak)
        row_total = jnp.sum(exp_scores, axis=-1, keepdims=True)
        weights = (exp_scores / row_total).astype(jnp.bfloat16)
        mix_block = jnp.einsum(
            "hqk,khd->qhd", weights, value_rows, preferred_element_type=jnp.float32
        )
        return (mix_block, (row_peak + jnp.log(row_total))[..., 0])

    starts_all = jnp.arange(block_count, dtype=jnp.int32) * BLOCK
    mix_blocks, log_total = lax.map(one_block, starts_all)
    return (mix_blocks.reshape(length, heads_here, head_size), log_total)


def attend_back(queries, key_rows, value_rows, segment, log_total, grad_mix, score_scale):
    length, heads_here, head_size = queries.shape
    block_count = length // BLOCK
    key_place = jnp.arange(length, dtype=jnp.int32)

    def one_block(running, block_item):
        first_row, block_total = block_item
        query_block = lax.dynamic_slice_in_dim(queries, first_row, BLOCK, 0)
        grad_block = lax.dynamic_slice_in_dim(grad_mix, first_row, BLOCK, 0)
        scores = block_scores(query_block, key_rows, segment, first_row, key_place, score_scale)
        weights = jnp.exp(scores - block_total[:, :, None])
        pull_rows = jnp.einsum(
            "qhd,khd->hqk", grad_block, value_rows, preferred_element_type=jnp.float32
        )
        inner = jnp.sum(weights * pull_rows, axis=-1, keepdims=True)
        grad_scores = (weights * (pull_rows - inner)).astype(jnp.bfloat16)
        query_part = (
            jnp.einsum("hqk,khd->qhd", grad_scores, key_rows, preferred_element_type=jnp.float32)
            * score_scale
        )
        key_part = (
            running[0]
            + jnp.einsum(
                "hqk,qhd->khd", grad_scores, query_block, preferred_element_type=jnp.float32
            )
            * score_scale
        )
        value_part = running[1] + jnp.einsum(
            "hqk,qhd->khd",
            weights.astype(jnp.bfloat16),
            grad_block,
            preferred_element_type=jnp.float32,
        )
        return ((key_part, value_part), query_part)

    starts_all = jnp.arange(block_count, dtype=jnp.int32) * BLOCK
    empty = jnp.zeros((length, heads_here, head_size), jnp.float32)
    (key_grad, value_grad), query_parts = lax.scan(
        one_block, (empty, empty), (starts_all, log_total)
    )
    return (query_parts.reshape(length, heads_here, head_size), key_grad, value_grad)


def local(
    inputs,
    segment_ids,
    cotangent,
    attn_norm_gain,
    attn_norm_bias,
    qkv_weight,
    qkv_bias,
    attn_sub_gain,
    attn_sub_bias,
    out_weight,
    out_bias,
    ffn_norm_gain,
    ffn_norm_bias,
    up_weight,
    up_bias,
    ffn_sub_gain,
    ffn_sub_bias,
    down_weight,
    down_bias,
):
    own_seqs, length, width = inputs.shape
    group_seqs = segment_ids.shape[0]
    own_count = own_seqs * length
    row_count = group_seqs * length
    local_width = qkv_weight.shape[2]
    local_heads = local_width // HD
    score_scale = HD ** (-0.5)
    head_shape = (group_seqs, length, local_heads, HD)
    gathered = (
        lax.all_gather(inputs, "tensor", axis=0, tiled=True),
        lax.all_gather(cotangent, "tensor", axis=0, tiled=True),
    )
    whole_input = gathered[0].reshape(row_count, width).astype(jnp.float32)
    whole_cot = gathered[1].reshape(row_count, width)
    unit_one, inv_one, normed_one = norm_rows(whole_input, attn_norm_gain, attn_norm_bias)
    normed_one = normed_one.astype(jnp.bfloat16)
    projected = (
        jnp.einsum("rd,jde->jre", normed_one, qkv_weight, preferred_element_type=jnp.float32)
        + qkv_bias[:, None, :]
    )
    token_place = positions(segment_ids)
    queries = rotate(projected[0].reshape(head_shape), token_place).astype(jnp.bfloat16)
    key_rows = rotate(projected[1].reshape(head_shape), token_place).astype(jnp.bfloat16)
    value_rows = projected[2].reshape(head_shape).astype(jnp.bfloat16)

    def forward_seq(operands):
        return attend_forward(operands[0], operands[1], operands[2], operands[3], score_scale)

    mixed, log_total = lax.map(forward_seq, (queries, key_rows, value_rows, segment_ids))
    mixed = mixed.reshape(row_count, local_width)
    mix_sums = lax.psum((jnp.sum(mixed, axis=-1), jnp.sum(mixed * mixed, axis=-1)), "tensor")
    unit_mix, inv_mix = shared_norm(mix_sums, mixed, width)
    sub_one = (unit_mix * attn_sub_gain + attn_sub_bias).astype(jnp.bfloat16)
    own_input = inputs.reshape(own_count, width).astype(jnp.float32)
    middle = (
        own_input
        + lax.psum_scatter(
            jnp.dot(sub_one, out_weight, preferred_element_type=jnp.float32),
            "tensor",
            scatter_dimension=0,
            tiled=True,
        )
        + out_bias
    )
    unit_two, inv_two, normed_two = norm_rows(middle, ffn_norm_gain, ffn_norm_bias)
    whole_two = lax.all_gather(normed_two.astype(jnp.bfloat16), "tensor", axis=0, tiled=True)
    hidden = jnp.dot(whole_two, up_weight, preferred_element_type=jnp.float32) + up_bias
    active, gelu_pull = jax.vjp(exact_gelu, hidden)
    act_sums = lax.psum((jnp.sum(active, axis=-1), jnp.sum(active * active, axis=-1)), "tensor")
    unit_act, inv_act = shared_norm(act_sums, active, FF)
    sub_two = (unit_act * ffn_sub_gain + ffn_sub_bias).astype(jnp.bfloat16)
    final = (
        middle
        + lax.psum_scatter(
            jnp.dot(sub_two, down_weight, preferred_element_type=jnp.float32),
            "tensor",
            scatter_dimension=0,
            tiled=True,
        )
        + down_bias
    )
    outputs = final.astype(jnp.bfloat16).reshape(inputs.shape)
    down_bias_grad = jnp.sum(whole_cot, axis=0, dtype=jnp.float32)
    down_weight_grad = jnp.einsum(
        "rf,rd->fd", sub_two, whole_cot, preferred_element_type=jnp.float32
    )
    grad_sub_two = jnp.einsum(
        "rd,fd->rf", whole_cot, down_weight, preferred_element_type=jnp.float32
    )
    ffn_sub_gain_grad = jnp.sum(grad_sub_two * unit_act, axis=0)
    ffn_sub_bias_grad = jnp.sum(grad_sub_two, axis=0)
    scaled_two = grad_sub_two * ffn_sub_gain
    back_sums = lax.psum(
        (jnp.sum(scaled_two, axis=-1), jnp.sum(scaled_two * unit_act, axis=-1)), "tensor"
    )
    grad_active = shared_back(back_sums, scaled_two, unit_act, inv_act, FF)
    grad_hidden = gelu_pull(grad_active)[0].astype(jnp.bfloat16)
    up_bias_grad = jnp.sum(grad_hidden, axis=0, dtype=jnp.float32)
    up_weight_grad = jnp.einsum(
        "rd,rf->df", whole_two, grad_hidden, preferred_element_type=jnp.float32
    )
    grad_norm_two = lax.psum_scatter(
        jnp.einsum("rf,df->rd", grad_hidden, up_weight, preferred_element_type=jnp.float32),
        "tensor",
        scatter_dimension=0,
        tiled=True,
    )
    own_cot = cotangent.reshape(own_count, width).astype(jnp.float32)
    grad_middle = own_cot + norm_back(grad_norm_two, unit_two, inv_two, ffn_norm_gain)
    gain_two_part = jnp.sum(grad_norm_two * unit_two, axis=0)
    bias_two_part = jnp.sum(grad_norm_two, axis=0)
    whole_mid = lax.all_gather(grad_middle.astype(jnp.bfloat16), "tensor", axis=0, tiled=True)
    out_bias_grad = jnp.sum(whole_mid, axis=0, dtype=jnp.float32)
    out_weight_grad = jnp.einsum(
        "re,rd->ed", sub_one, whole_mid, preferred_element_type=jnp.float32
    )
    grad_sub_one = jnp.einsum(
        "rd,ed->re", whole_mid, out_weight, preferred_element_type=jnp.float32
    )
    attn_sub_gain_grad = jnp.sum(grad_sub_one * unit_mix, axis=0)
    attn_sub_bias_grad = jnp.sum(grad_sub_one, axis=0)
    scaled_one = grad_sub_one * attn_sub_gain
    mix_back = lax.psum(
        (
            jnp.sum(scaled_one, axis=-1),
            jnp.sum(scaled_one * unit_mix, axis=-1),
            gain_two_part,
            bias_two_part,
        ),
        "tensor",
    )
    ffn_norm_gain_grad = mix_back[2]
    ffn_norm_bias_grad = mix_back[3]
    grad_mix = shared_back((mix_back[0], mix_back[1]), scaled_one, unit_mix, inv_mix, width)
    grad_mix = grad_mix.astype(jnp.bfloat16).reshape(head_shape)

    def backward_seq(operands):
        return attend_back(
            operands[0],
            operands[1],
            operands[2],
            operands[3],
            operands[4],
            operands[5],
            score_scale,
        )

    query_grad, key_grad, value_grad = lax.map(
        backward_seq, (queries, key_rows, value_rows, segment_ids, log_total, grad_mix)
    )
    stacked = jnp.stack(
        [unrotate(query_grad, token_place), unrotate(key_grad, token_place), value_grad]
    )
    stacked = stacked.astype(jnp.bfloat16).reshape(3, row_count, local_width)
    qkv_bias_grad = jnp.sum(stacked, axis=1, dtype=jnp.float32)
    qkv_weight_grad = jnp.einsum(
        "rd,jre->jde", normed_one, stacked, preferred_element_type=jnp.float32
    )
    grad_norm_one = lax.psum(
        jnp.einsum("jre,jde->rd", stacked, qkv_weight, preferred_element_type=jnp.float32), "tensor"
    )
    attn_norm_gain_grad = jnp.sum(grad_norm_one * unit_one, axis=0)
    attn_norm_bias_grad = jnp.sum(grad_norm_one, axis=0)
    first_own = lax.axis_index("tensor") * own_count
    own_grad_norm = lax.dynamic_slice_in_dim(grad_norm_one, first_own, own_count, 0)
    own_unit = lax.dynamic_slice_in_dim(unit_one, first_own, own_count, 0)
    own_inv = lax.dynamic_slice_in_dim(inv_one, first_own, own_count, 0)
    input_grad = (
        grad_middle + norm_back(own_grad_norm, own_unit, own_inv, attn_norm_gain)
    ).reshape(inputs.shape)
    summed = lax.psum(
        (
            attn_norm_gain_grad,
            attn_norm_bias_grad,
            qkv_weight_grad,
            qkv_bias_grad,
            attn_sub_gain_grad,
            attn_sub_bias_grad,
            out_weight_grad,
            out_bias_grad,
            ffn_norm_gain_grad,
            ffn_norm_bias_grad,
            up_weight_grad,
            up_bias_grad,
            ffn_sub_gain_grad,
            ffn_sub_bias_grad,
            down_weight_grad,
            down_bias_grad,
        ),
        "dp",
    )
    return (
        outputs,
        input_grad,
        summed[0],
        summed[1],
        summed[2],
        summed[3],
        summed[4],
        summed[5],
        summed[6],
        summed[7],
        summed[8],
        summed[9],
        summed[10],
        summed[11],
        summed[12],
        summed[13],
        summed[14],
        summed[15],
    )


def solution(mesh):
    in_specs = (
        P(("dp", "tensor"), None, None),
        P("dp", None),
        P(("dp", "tensor"), None, None),
        P(),
        P(),
        P(None, None, "tensor"),
        P(None, "tensor"),
        P("tensor"),
        P("tensor"),
        P("tensor", None),
        P(),
        P(),
        P(),
        P(None, "tensor"),
        P("tensor"),
        P("tensor"),
        P("tensor"),
        P("tensor", None),
        P(),
    )
    out_specs = (
        P(("dp", "tensor"), None, None),
        P(("dp", "tensor"), None, None),
        P(),
        P(),
        P(None, None, "tensor"),
        P(None, "tensor"),
        P("tensor"),
        P("tensor"),
        P("tensor", None),
        P(),
        P(),
        P(),
        P(None, "tensor"),
        P("tensor"),
        P("tensor"),
        P("tensor"),
        P("tensor", None),
        P(),
    )
    return jax.shard_map(local, mesh=mesh, in_specs=in_specs, out_specs=out_specs, check_vma=False)
```

profile of v0, /device:TPU:0, one launch (start us, length us, event | category | flops | bytes accessed | tf_op | source)
XLA Modules:
  0.0 1235.4 jit_solution(18235471978319214233)
XLA Ops:
  14.7 9.8 all-gather.5.cloned.1.call-done
  44.2 5.6 reshape_squeeze.7
  53.3 5.6 reshape_squeeze.8
  58.9 5.5 subtract_convert_fusion.2
  81.4 89.6 %while.55 = (s32[]{:T(128)}, f32[2,1024,6,64]{3,2,1,0:T(8,128)}, f32[2,2,6,512]{3,2,1,0:T(8,128)S(1)}, bf16[2,1024,6,64]{1,3,2,0:T(8,128)(2,1)}, s32[2,1024]{1,0...) while((s32[]{:T(128)}, f32[2,1024,6,64]{3,2,1,0:T(8,128)}, ...), condition=%wide.region_9.10_spmd, body=%wide.region_4.9_spmd.sunk | while | flops 844625408 | bytes 68488648 | solution.py:216
  84.9 32.8 %while.58 = (s32[]{:T(128)}, f32[2,512,6,64]{1,3,2,0:T(8,128)}, f32[2,6,512]{2,1,0:T(8,128)S(1)}, s32[2]{0:T(128)S(1)}, s32[1024]{0:T(1024)S(1)}, /*index=5*/bf1...) while((s32[]{:T(128)}, f32[2,512,6,64]{1,3,2,0:T(8,128)}, ...), condition=%wide.region_8.8_spmd.clone, body=%wide.region_5.7_spmd.clone.sunk | while | flops 844625408 | bytes 45869764 | solution.py:120
  96.4 4.9 fusion.128
  112.8 4.9 fusion.128
  129.6 32.8 %while.58 = (s32[]{:T(128)}, f32[2,512,6,64]{1,3,2,0:T(8,128)}, f32[2,6,512]{2,1,0:T(8,128)S(1)}, s32[2]{0:T(128)S(1)}, s32[1024]{0:T(1024)S(1)}, /*index=5*/bf1...) while((s32[]{:T(128)}, f32[2,512,6,64]{1,3,2,0:T(8,128)}, ...), condition=%wide.region_8.8_spmd.clone, body=%wide.region_5.7_spmd.clone.sunk | while | flops 844625408 | bytes 45869764 | solution.py:120
  141.0 4.9 fusion.128
  157.4 4.9 fusion.128
  171.0 12.7 %fusion.56 = (f32[2,1024]{1,0:T(2,128)S(1)}, f32[2,1024]{1,0:T(2,128)S(1)}) fusion(f32[2,1024,6,64]{3,2,1,0:T(8,128)} %get-tuple-element.222), kind=kLoop, calls=%fused_computation.172 | loop fusion | flops 2355200 | bytes 3162112 | tf_op jit(solution)/shard_map/reduce_sum | solution.py:218
  183.7 7.2 reshape.399
  194.8 6.4 fusion.54
  202.3 14.5 %reduce-scatter.4.cloned.1.call-done = f32[1024,768]{1,0:T(8,128)} async-done(((f32[2048,768]{1,0:T(8,128)}), f32[1024,768]{1,0:T(8,128)}) %reduce-scatter.4.cloned.1.call-update) | async-done | bytes 3145744 | tf_op jit(solution)/shard_map/reduce_scatter | solution.py:224
  223.2 9.2 all-gather.9.cloned.1.call-done
  232.5 10.7 fusion.63
  243.2 12.9 %copy.96 = f32[2048,1536]{0,1:T(8,128)} copy(f32[2048,1536]{1,0:T(8,128)} %get-tuple-element.556) | data formatting | bytes 25165824 | tf_op jit(solution)/shard_map/rd,fd->rf/dot_general | solution.py:254
  256.1 37.5 %fusion.55 = (f32[2048]{0:T(1024)S(1)}, f32[2048]{0:T(1024)S(1)}, f32[2048,1536]{0,1:T(8,128)}, f32[2048,1536]{0,1:T(8,128)}, f32[2048,1536]{0,1:T(8,128)}) fusion(f32[1536]{0:T(1024)S(1)} %copy-done.59, bf16[2048,768]{1,0:T(8,128)(2,1)} %all-gather.7.cloned.1.call-done, bf16[768,1536]{1,0:T(8,128)(2,1)S(1)} %copy-done), kind=kOutput, calls=%fused_computation.171 | convolution fusion | flops 5045743616 | bytes 43276288 | tf_op jit(solution)/shard_map/dot_general | solution.py:234
  297.0 10.6 multiply_reduce_fusion.1
  311.5 21.4 %convert_reduce_fusion = (f32[1536]{0:T(1024)}, bf16[2048,1536]{0,1:T(8,128)(2,1)S(1)}, bf16[2048,1536]{0,1:T(8,128)(2,1)}) fusion(f32[2048,1536]{0,1:T(8,128)} %get-tuple-element.514, f32[2048]{0:T(1024)S(1)} %broadcast_multiply_fusion, f32[2048,1536]{0,1:T(8,128)} %get-tuple-element.513, f32[2048]{0:T(1024)S(1)} %get-tuple-element.547, ...), kind=kLoop, calls=%fused_computation.64 | loop fusion | flops 84933120 | bytes 62971904 | tf_op jit(solution)/shard_map/reduce_sum | solution.py:265
  335.5 7.0 fusion.65
  344.2 10.1 fusion.64
  361.5 14.6 %reduce-scatter.6.cloned.1.call-done = f32[1024,768]{1,0:T(8,128)} async-done(((f32[2048,768]{1,0:T(8,128)}), f32[1024,768]{1,0:T(8,128)}) %reduce-scatter.6.cloned.1.call-update) | async-done | bytes 3145744 | tf_op jit(solution)/shard_map/reduce_scatter | solution.py:241
  376.1 6.1 fusion.59
  382.4 14.2 %all-gather.11.cloned.1.call-done = bf16[2048,768]{1,0:T(8,128)(2,1)} async-done(((bf16[1024,768]{1,0:T(8,128)(2,1)}), bf16[2048,768]{1,0:T(8,128)(2,1)}) %all-gather.11.cloned.1.call-update) | async-done | bytes 3145744 | tf_op jit(solution)/shard_map/all_gather | solution.py:279
  396.6 7.3 multiply_reduce_fusion.9
  419.5 317.4 %while.57 = (s32[]{:T(128)}, f32[2,1024,6,64]{1,0,3,2:T(2,128)}, f32[2,1024,6,64]{1,0,3,2:T(2,128)}, bf16[2,1024,6,64]{1,3,2,0:T(8,128)(2,1)}, f32[2,2,6,512]{3,...) while((s32[]{:T(128)}, f32[2,1024,6,64]{1,0,3,2:T(2,128)}, ...), condition=%wide.region_37.38_spmd, body=%wide.region_33.37_spmd.sunk | while | flops 2064184832 | bytes 271224064 | solution.py:315
  424.6 82.1 %while.59 = (s32[]{:T(128)}, f32[1024,6,64]{0,2,1:T(8,128)}, f32[1024,6,64]{0,2,1:T(8,128)}, f32[2,512,6,64]{1,3,2,0:T(8,128)}, s32[2]{0:T(128)S(1)}, /*index=5*...) while((s32[]{:T(128)}, f32[1024,6,64]{0,2,1:T(8,128)}, ...), condition=%wide.region_36.36_spmd.clone, body=%wide.region_34.35_spmd.clone.sunk | while | flops 2064184832 | bytes 214543200 | solution.py:161
  430.4 8.1 multiply_reduce_fusion.17
  438.7 9.6 multiply_convert_fusion.3
  448.3 5.4 bitcast_add_fusion.4
  453.6 6.3 fusion.122
  470.6 8.1 multiply_reduce_fusion.17
  478.9 9.6 multiply_convert_fusion.3
  488.5 5.8 bitcast_add_fusion.4
  494.3 6.3 fusion.122
  500.6 6.0 bitcast_add_fusion.5
  510.4 6.7 copy.174
  517.1 27.8 %dynamic_update_slice.48 = f32[2,1024,6,64]{1,0,3,2:T(2,128)} dynamic-update-slice(f32[2,1024,6,64]{1,0,3,2:T(2,128)} %get-tuple-element.976, f32[1,1024,6,64]{1,0,3,2:T(1,128)} %copy.174, s32[]{:T(128)} %get-tuple-element.975, s32[]{:T(128)} %constant.91.clone.1..sunk.2, s32[]{:T(128)} %constant.91.clone.1..sunk.2, s32[]{:T(128)} %constant.91.clone.1..sunk.2) | dynamic-update-slice | bytes 3145732 | tf_op jit(solution)/shard_map/while/body/jit(dynamic_update_index_in_dim)/dynamic_update_slice | solution.py:216
  547.6 27.9 %dynamic_update_slice.49 = f32[2,1024,6,64]{1,0,3,2:T(2,128)} dynamic-update-slice(f32[2,1024,6,64]{1,0,3,2:T(2,128)} %get-tuple-element.977, f32[1,1024,6,64]{1,0,3,2:T(1,128)} %copy.175, s32[]{:T(128)} %get-tuple-element.975, s32[]{:T(128)} %constant.91.clone.1..sunk.2, s32[]{:T(128)} %constant.91.clone.1..sunk.2, s32[]{:T(128)} %constant.91.clone.1..sunk.2) | dynamic-update-slice | bytes 3145732 | tf_op jit(solution)/shard_map/while/body/jit(dynamic_update_index_in_dim)/dynamic_update_slice | solution.py:216
  583.0 82.1 %while.59 = (s32[]{:T(128)}, f32[1024,6,64]{0,2,1:T(8,128)}, f32[1024,6,64]{0,2,1:T(8,128)}, f32[2,512,6,64]{1,3,2,0:T(8,128)}, s32[2]{0:T(128)S(1)}, /*index=5*...) while((s32[]{:T(128)}, f32[1024,6,64]{0,2,1:T(8,128)}, ...), condition=%wide.region_36.36_spmd.clone, body=%wide.region_34.35_spmd.clone.sunk | while | flops 2064184832 | bytes 214543200 | solution.py:161
  588.9 8.1 multiply_reduce_fusion.17
  597.1 9.6 multiply_convert_fusion.3
  606.7 5.4 bitcast_add_fusion.4
  612.1 6.3 fusion.122
  629.1 8.1 multiply_reduce_fusion.17
  637.3 9.6 multiply_convert_fusion.3
  646.9 5.8 bitcast_add_fusion.4
  652.8 6.3 fusion.122
  659.1 6.0 bitcast_add_fusion.5
  668.8 6.7 copy.174
  675.5 27.8 %dynamic_update_slice.48 = f32[2,1024,6,64]{1,0,3,2:T(2,128)} dynamic-update-slice(f32[2,1024,6,64]{1,0,3,2:T(2,128)} %get-tuple-element.976, f32[1,1024,6,64]{1,0,3,2:T(1,128)} %copy.174, s32[]{:T(128)} %get-tuple-element.975, s32[]{:T(128)} %constant.91.clone.1..sunk.2, s32[]{:T(128)} %constant.91.clone.1..sunk.2, s32[]{:T(128)} %constant.91.clone.1..sunk.2) | dynamic-update-slice | bytes 3145732 | tf_op jit(solution)/shard_map/while/body/jit(dynamic_update_index_in_dim)/dynamic_update_slice | solution.py:216
  706.0 27.9 %dynamic_update_slice.49 = f32[2,1024,6,64]{1,0,3,2:T(2,128)} dynamic-update-slice(f32[2,1024,6,64]{1,0,3,2:T(2,128)} %get-tuple-element.977, f32[1,1024,6,64]{1,0,3,2:T(1,128)} %copy.175, s32[]{:T(128)} %get-tuple-element.975, s32[]{:T(128)} %constant.91.clone.1..sunk.2, s32[]{:T(128)} %constant.91.clone.1..sunk.2, s32[]{:T(128)} %constant.91.clone.1..sunk.2) | dynamic-update-slice | bytes 3145732 | tf_op jit(solution)/shard_map/while/body/jit(dynamic_update_index_in_dim)/dynamic_update_slice | solution.py:216
  737.0 5.4 add_convert_fusion.7
  768.9 9.4 convolution_bitcast_fusion
  778.5 9.8 fusion.67
  788.3 11.3 fusion.66
  802.6 6.1 convolution_bitcast_fusion.1
  820.3 82.5 %all-reduce = (f32[768]{0:T(1024)}, f32[768]{0:T(1024)}, f32[3,384]{1,0:T(4,128)}, f32[384]{0:T(512)}, f32[384]{0:T(512)}, /*index=5*/f32[768]{0:T(1024)}, f32[7...) all-reduce(f32[768]{0:T(1024)S(1)} %get-tuple-element.402, ...), channel_id=1, replica_groups=mesh['dp'=16,'tensor'=2] {'dp'}, use_global_device_ids=true, to_apply=%region_42.43 | all-reduce | flops 11136 | bytes 89088 | tf_op jit(solution)/shard_map/psum | solution.py:338
  907.8 4.9 add_bitcast_fusion.1
  912.7 302.0 %all-reduce.11.cloned.1.call-done = (f32[3,768,384]{1,2,0:T(8,128)}, f32[384,768]{1,0:T(8,128)}, f32[768,1536]{1,0:T(8,128)}, f32[1536,768]{1,0:T(8,128)}) async-done(((f32[3,768,384]{1,2,0:T(8,128)}, f32[384,768]{1,0:T(8,128)}, f32[768,1536]{1,0:T(8,128)}, f32[1536,768]{1,0:T(8,128)}), (f32[3,768,384]{1,2,0:T(8,128)}, f32[384,768]{1,0:T(8,128)}, f32[768,1536]{1,0:T(8,128)}, ...) | async-done | bytes 14155792 | tf_op jit(solution)/shard_map/psum | solution.py:338
  1214.7 5.2 copy.114
  1221.0 5.5 copy.234
  (391 shorter events, 257.5 us)
Async XLA Ops:
  7.2 248.9 %copy-start = (bf16[768,1536]{1,0:T(8,128)(2,1)S(1)}, bf16[768,1536]{1,0:T(8,128)(2,1)}, u32[]{:S(2)}) copy-start(bf16[768,1536]{1,0:T(8,128)(2,1)} %param.40) | copy-start | bytes 7077892
  7.2 17.2 %all-gather.5.cloned.1.call-start = ((), (), s32[]{:S(2)}) async-start(), calls=%async_computation.3 | async-start | bytes 4718592 | tf_op jit(solution)/shard_map/all_gather | solution.py:197
  7.9 208.8 %reduce-scatter.4.cloned.1.call-start = ((), (), s32[]{:S(2)}) async-start(), calls=%async_computation.4 | async-start | bytes 9437184 | tf_op jit(solution)/shard_map/reduce_scatter | solution.py:224
  14.6 44.2 %copy-start.23 = (f32[2,1024,32]{1,0,2:T(2,128)}, f32[2,1024,32]{1,0,2:T(2,128)S(1)}, u32[]{:S(2)}) copy-start(f32[2,1024,32]{1,0,2:T(2,128)S(1)} %get-tuple-element.542) | copy-start | bytes 786436
  14.6 44.2 %copy-start.24 = (f32[2,1024,32]{1,0,2:T(2,128)}, f32[2,1024,32]{1,0,2:T(2,128)S(1)}, u32[]{:S(2)}) copy-start(f32[2,1024,32]{1,0,2:T(2,128)S(1)} %get-tuple-element.543) | copy-start | bytes 786436
  74.5 6.9 copy-start.36
  171.0 12.7 %copy-start.37 = (f32[2,2,6,512]{3,2,1,0:T(8,128)}, f32[2,2,6,512]{3,2,1,0:T(8,128)S(1)}, u32[]{:S(2)}) copy-start(f32[2,2,6,512]{3,2,1,0:T(8,128)S(1)} %get-tuple-element.964) | copy-start | bytes 147460
  183.7 11.1 copy-start.28
  183.7 11.1 copy-start.38
  183.7 11.1 copy-start.49
  201.3 15.5 %copy-start.62 = (f32[768]{0:T(1024)S(1)}, f32[768]{0:T(1024)}, u32[]{:S(2)}) copy-start(f32[768]{0:T(1024)} %param.37) | copy-start | bytes 9220
  201.3 31.2 %all-gather.9.cloned.1.call-start = ((), (), s32[]{:S(2)}) async-start(), calls=%async_computation.7 | async-start | bytes 4718592 | tf_op jit(solution)/shard_map/all_gather | solution.py:198
  202.0 19.4 %copy-start.51 = (f32[768]{0:T(1024)S(1)}, f32[768]{0:T(1024)}, u32[]{:S(2)}) copy-start(f32[768]{0:T(1024)} %param.38) | copy-start | bytes 9220
  202.0 19.4 %copy-start.63 = (f32[768]{0:T(1024)S(1)}, f32[768]{0:T(1024)}, u32[]{:S(2)}) copy-start(f32[768]{0:T(1024)} %param.39) | copy-start | bytes 9220
  202.0 54.1 %all-gather.7.cloned.1.call-start = ((), (), s32[]{:S(2)}) async-start(), calls=%async_computation.5 | async-start | bytes 4718592 | tf_op jit(solution)/shard_map/all_gather | solution.py:233
  223.2 134.7 %reduce-scatter.8.cloned.1.call-start = ((), (), s32[]{:S(2)}) async-start(), calls=%async_computation.8 | async-start | bytes 9437184 | tf_op jit(solution)/shard_map/reduce_scatter | solution.py:269
  243.2 12.9 %copy-start.59 = (f32[1536]{0:T(1024)S(1)}, f32[1536]{0:T(1024)}, u32[]{:S(2)}) copy-start(f32[1536]{0:T(1024)} %param.41) | copy-start | bytes 18436
  256.1 40.9 %copy-start.53 = (f32[1536]{0:T(1024)S(1)}, f32[1536]{0:T(1024)}, u32[]{:S(2)}) copy-start(f32[1536]{0:T(1024)} %param.42) | copy-start | bytes 18436
  297.0 14.5 %copy-start.60 = (f32[1536]{0:T(1024)S(1)}, f32[1536]{0:T(1024)}, u32[]{:S(2)}) copy-start(f32[1536]{0:T(1024)} %param.43) | copy-start | bytes 18436
  342.5 33.6 %reduce-scatter.6.cloned.1.call-start = ((), (), s32[]{:S(2)}) async-start(), calls=%async_computation.6 | async-start | bytes 9437184 | tf_op jit(solution)/shard_map/reduce_scatter | solution.py:241
  354.3 21.9 %copy-start.18 = (bf16[1,1024,768]{2,1,0:T(8,128)(2,1)S(1)}, bf16[1,1024,768]{2,1,0:T(8,128)(2,1)}, u32[]{:S(2)}) copy-start(bf16[1,1024,768]{2,1,0:T(8,128)(2,1)} %param.29) | copy-start | bytes 4718596
  354.3 21.8 %copy-start.64 = (f32[768]{0:T(1024)S(1)}, f32[768]{0:T(1024)}, u32[]{:S(2)}) copy-start(f32[768]{0:T(1024)} %param.45) | copy-start | bytes 9220
  354.3 42.3 %all-gather.11.cloned.1.call-start = ((), (), s32[]{:S(2)}) async-start(), calls=%async_computation.9 | async-start | bytes 4718592 | tf_op jit(solution)/shard_map/all_gather | solution.py:279
  361.5 35.1 %copy-start.29 = (bf16[384,768]{1,0:T(8,128)(2,1)S(1)}, bf16[384,768]{1,0:T(8,128)(2,1)}, u32[]{:S(2)}) copy-start(bf16[384,768]{1,0:T(8,128)(2,1)} %param.36) | copy-start | bytes 1769476
  361.5 35.1 %copy-start.31 = (f32[2048]{0:T(1024)S(1)}, f32[2048]{0:T(1024)}, u32[]{:S(2)}) copy-start(f32[2048]{0:T(1024)} %copy-done.30) | copy-start | bytes 24580
  361.5 35.1 %copy-start.34 = (f32[2048]{0:T(1024)S(1)}, f32[2048]{0:T(1024)}, u32[]{:S(2)}) copy-start(f32[2048]{0:T(1024)} %copy-done.33) | copy-start | bytes 24580
  361.5 35.1 %copy-start.39 = (f32[384]{0:T(512)S(1)}, f32[384]{0:T(512)}, u32[]{:S(2)}) copy-start(f32[384]{0:T(512)} %param.34) | copy-start | bytes 4612
  382.3 433.2 %all-reduce.9.cloned.1.call-start = ((), (), s32[]{:S(2)}) async-start(), calls=%async_computation.10 | async-start | bytes 12582912 | tf_op jit(solution)/shard_map/psum | solution.py:326
  430.4 8.3 copy-start.2
  448.3 11.7 copy-start.3
  453.6 6.3 copy-start.6
  470.6 8.3 copy-start.2
  488.5 12.1 copy-start.3
  494.3 6.3 copy-start.6
  510.4 34.4 %copy-start.4 = (f32[1024,6,64]{0,2,1:T(8,128)S(1)}, f32[1024,6,64]{0,2,1:T(8,128)}, u32[]{:S(2)}) copy-start(f32[1024,6,64]{0,2,1:T(8,128)} %get-tuple-element.822) | copy-start | bytes 4718596 | tf_op jit(solution)/shard_map/while
  547.6 27.9 %copy-start.25 = (bf16[2,1024,6,64]{1,3,2,0:T(8,128)(2,1)S(1)}, bf16[2,1024,6,64]{1,3,2,0:T(8,128)(2,1)}, u32[]{:S(2)}) copy-start(bf16[2,1024,6,64]{1,3,2,0:T(8,128)(2,1)} %get-tuple-element.978) | copy-start | bytes 4718596 | tf_op jit(solution)/shard_map/while
  588.8 8.3 copy-start.2
  606.7 11.7 copy-start.3
  612.1 6.3 copy-start.6
  629.0 8.3 copy-start.2
  646.9 12.1 copy-start.3
  652.8 6.3 copy-start.6
  668.8 34.4 %copy-start.4 = (f32[1024,6,64]{0,2,1:T(8,128)S(1)}, f32[1024,6,64]{0,2,1:T(8,128)}, u32[]{:S(2)}) copy-start(f32[1024,6,64]{0,2,1:T(8,128)} %get-tuple-element.822) | copy-start | bytes 4718596 | tf_op jit(solution)/shard_map/while
  706.0 27.9 %copy-start.25 = (bf16[2,1024,6,64]{1,3,2,0:T(8,128)(2,1)S(1)}, bf16[2,1024,6,64]{1,3,2,0:T(8,128)(2,1)}, u32[]{:S(2)}) copy-start(bf16[2,1024,6,64]{1,3,2,0:T(8,128)(2,1)} %get-tuple-element.978) | copy-start | bytes 4718596 | tf_op jit(solution)/shard_map/while
  778.4 436.3 %all-reduce.11.cloned.1.call-start = ((), (), s32[]{:S(2)}) async-start(), calls=%async_computation.11 | async-start | bytes 28311552 | tf_op jit(solution)/shard_map/psum | solution.py:338
  778.4 9.8 copy-start.69
  778.4 24.1 %slice-start = ((s8[6291456]{0:T(1024)(128)(4,1)}), s8[4194304]{0:T(1024)(128)(4,1)S(1)}, s32[]{:S(2)}) async-start(s8[6291456]{0:T(1024)(128)(4,1)} %bitcast.216), calls=%async_computation.12 | async-start | bytes 8388608
  788.2 11.3 copy-start.7
  788.2 11.3 copy-start.16
  788.3 11.3 copy-start.32
  788.3 11.3 copy-start.35
  788.3 11.3 copy-start.40
  788.3 11.3 copy-start.50
  788.3 14.3 %slice-start.1 = ((s8[6291456]{0:T(1024)(128)(4,1)}), s8[2097152]{0:T(1024)(128)(4,1)S(1)}, s32[]{:S(2)}) async-start(s8[6291456]{0:T(1024)(128)(4,1)} %bitcast.216), calls=%async_computation.13 | async-start | bytes 4194304
  809.4 5.2 copy-start.20
  809.4 5.2 copy-start.22
  815.4 4.8 copy-start.54
  815.4 4.8 copy-start.55
  815.4 4.8 copy-start.61
  902.7 5.1 copy-start.13
  1214.7 5.3 copy-start.27
  1220.0 6.5 slice-start.2
  1221.0 5.5 slice-start.3
  1221.0 7.7 copy-start.1
  (45 other events, 116.3 us)
Sparse Core Ops, SparseCore 0:
  9.6 14.8 all-gather.4
  201.4 15.2 reduce-scatter.3
  218.3 14.1 all-gather.8
  234.4 13.2 all-gather.6
  342.6 15.1 reduce-scatter.7
  360.0 16.0 reduce-scatter.5
  382.4 14.1 all-gather.10
  778.5 33.4 all-reduce.8
  820.1 394.5 all-reduce.10
where the time goes:
time: 1250 us; the launch traced here: 1240 us
  waiting for transfers between devices  369 us (30%)
  local copies, waits for them, and re-layouts  292 us (23%)
  matrix products  268 us (21%)
  other arithmetic  177 us (14%)
  blocking collectives  97 us (8%)
  loops' own time  17.1 us (1%)
  between operations  15 us (1%)
    psum x1, waiting for transfers between devices, local(): lax.psum((attn_norm_gain_grad, attn_norm_bias_grad, qkv_weight_grad, qkv_...  302 us
    dynamic_update_slice x14, local copies, waits for them, and re-layouts, local(): lax.map(forward_seq, (queries, key_rows, value_rows, segment_ids))  142 us
    psum x1, blocking collectives, local(): lax.psum((attn_norm_gain_grad, attn_norm_bias_grad, qkv_weight_grad, qkv_...  82.5 us
    convert_element_type x4, other arithmetic, one_block(): grad_scores = (weights * (pull_rows - inner)).astype(jnp.bfloat16)  38.4 us
    dot_general x1, matrix products, local(): jnp.dot(whole_two, up_weight, preferred_element_type=jnp.float32) + up_bias  37.5 us
    dot_general x4, matrix products, one_block(): jnp.einsum('qhd,khd->hqk', grad_block, value_rows, preferred_element_type...  32.5 us
    unnamed x145, local copies, waits for them, and re-layouts  25.5 us
    dot_general x4, matrix products, one_block(): jnp.einsum('hqk,khd->qhd', grad_scores, key_rows, preferred_element_type=...  25.2 us
  transfers between devices with their start and end apart: 9, of which 7 were waited for; matrix products, arithmetic and copies ran while one was open for 8% of the time, Pallas kernels for 0%

commit v1 on v0

v1 whole, which is shorter than its diff:
```python
import math

import jax
import jax.numpy as jnp
from jax import lax
from jax.experimental import pallas as pl
from jax.experimental.pallas import tpu as pltpu
from jax.sharding import PartitionSpec as P

HD = 64
PAIR = 2 * HD
TILE = 256
REACH = 512
F32 = jnp.float32
BF16 = jnp.bfloat16
VMEM_BYTES = 60 * 1024 * 1024


def nn(a, b):
    return jnp.dot(a, b, preferred_element_type=F32)


def nt(a, b):
    return lax.dot_general(a, b, (((1,), (1,)), ((), ())), preferred_element_type=F32)


def tn(a, b):
    return lax.dot_general(a, b, (((0,), (0,)), ((), ())), preferred_element_type=F32)


def unit_rows(values):
    center = jnp.mean(values, axis=-1, keepdims=True)
    spread = jnp.mean(values * values, axis=-1, keepdims=True) - center * center
    inv = lax.rsqrt(spread + 1e-05)
    return (values - center) * inv, inv


def norm_back(grad, unit, inv, gain):
    scaled = grad * gain
    return inv * (
        scaled
        - jnp.mean(scaled, axis=-1, keepdims=True)
        - unit * jnp.mean(scaled * unit, axis=-1, keepdims=True)
    )


def swap_halves(values):
    lane = lax.broadcasted_iota(jnp.int32, values.shape, 1)
    return jnp.where(
        (lane & (HD // 2)) == 0,
        pltpu.roll(values, PAIR - HD // 2, axis=1),
        pltpu.roll(values, HD // 2, axis=1),
    )


def add_rows(ref, values):
    total = jnp.sum(values, axis=0, keepdims=True)

    @pl.when(pl.program_id(0) == 0)
    def _():
        ref[...] = total

    @pl.when(pl.program_id(0) != 0)
    def _():
        ref[...] += total


def project_kernel(
    x_ref, gain_ref, bias_ref, own_ref, oth_ref, qb_ref, cos_ref, sin_ref, n_ref, q_ref, k_ref, v_ref
):
    unit, _ = unit_rows(x_ref[...].astype(F32))
    normed = (unit * gain_ref[...] + bias_ref[...]).astype(BF16)
    n_ref[...] = normed
    half = own_ref.shape[2]
    cos = cos_ref[...]
    sin = sin_ref[...]
    for j, out_ref in enumerate((q_ref, k_ref, v_ref)):
        for side, w_ref in enumerate((own_ref, oth_ref)):
            pre = nn(normed, w_ref[j]) + qb_ref[j : j + 1, side * half : (side + 1) * half]
            for c in range(half // PAIR):
                part = pre[:, c * PAIR : (c + 1) * PAIR]
                if j < 2:
                    part = part * cos + swap_halves(part) * sin
                part = part.astype(BF16)
                if j == 0:
                    part = part * jnp.asarray(HD**-0.5, BF16)
                at = side * half + c * PAIR
                out_ref[:, at : at + PAIR] = part


def key_range(i):
    return max(0, i * TILE - REACH), (i + 1) * TILE


def head_masks(rows):
    lane = lax.broadcasted_iota(jnp.int32, (rows, PAIR), 1)
    return lane < HD, lane >= HD


def only(mask, values):
    return jnp.where(mask, values, jnp.zeros_like(values))


def attend_kernel(q_ref, k_ref, v_ref, scol_ref, srow_ref, mix_ref, lse_ref, bias_ref):
    blocks = q_ref.shape[0] // TILE

    @pl.when(pl.program_id(0) == 0)
    def _():
        at = 0
        for i in range(blocks):
            k0, k1 = key_range(i)
            shape = (TILE, k1 - k0)
            qi = lax.broadcasted_iota(jnp.int32, shape, 0) + i * TILE
            ki = lax.broadcasted_iota(jnp.int32, shape, 1) + k0
            keep = (scol_ref[i * TILE : (i + 1) * TILE, :] == srow_ref[:, k0:k1]) & (qi >= ki)
            bias_ref[:, at : at + k1 - k0] = jnp.where(keep, 0.0, -1e30).astype(F32)
            at += k1 - k0

    at = 0
    for i in range(blocks):
        k0, k1 = key_range(i)
        width = k1 - k0
        bias = bias_ref[:, at : at + width]
        at += width
        q = q_ref[i * TILE : (i + 1) * TILE, :]
        keys = k_ref[k0:k1, :]
        values = v_ref[k0:k1, :]
        qm = head_masks(TILE)
        km = head_masks(width)
        mixes = []
        lses = []
        for h in range(2):
            scores = nt(only(qm[h], q), keys) + bias
            peak = jnp.max(scores, axis=-1, keepdims=True)
            e = jnp.exp(scores - peak)
            total = jnp.sum(e, axis=-1, keepdims=True)
            weights = (e * (1.0 / total)).astype(BF16)
            mixes.append(nn(weights, only(km[h], values)))
            lses.append(peak + jnp.log(total))
        mix_ref[i * TILE : (i + 1) * TILE, :] = mixes[0] + mixes[1]
        both = jnp.where(
            qm[0], jnp.broadcast_to(lses[0], (TILE, PAIR)), jnp.broadcast_to(lses[1], (TILE, PAIR))
        )
        flipped = both.T
        lse_ref[0, 0:1, i * TILE : (i + 1) * TILE] = flipped[0:1]
        lse_ref[0, 1:2, i * TILE : (i + 1) * TILE] = flipped[HD : HD + 1]


def attend_back_kernel(
    q_ref, k_ref, v_ref, g_ref, lse_ref, scol_ref, srow_ref, cos_ref, sin_ref,
    dq_ref, dk_ref, dv_ref, bq_ref, bk_ref, bv_ref, bias_ref, ka_ref, va_ref,
):
    blocks = q_ref.shape[0] // TILE

    @pl.when(pl.program_id(0) == 0)
    def _():
        at = 0
        for i in range(blocks):
            k0, k1 = key_range(i)
            shape = (k1 - k0, TILE)
            ki = lax.broadcasted_iota(jnp.int32, shape, 0) + k0
            qi = lax.broadcasted_iota(jnp.int32, shape, 1) + i * TILE
            keep = (scol_ref[k0:k1, :] == srow_ref[:, i * TILE : (i + 1) * TILE]) & (qi >= ki)
            bias_ref[at : at + k1 - k0, :] = jnp.where(keep, 0.0, -1e30).astype(F32)
            at += k1 - k0

    ka_ref[...] = jnp.zeros_like(ka_ref)
    va_ref[...] = jnp.zeros_like(va_ref)

    def turn_back(values, rows):
        return values * cos_ref[rows, :] - swap_halves(values) * sin_ref[rows, :]

    sums_q = jnp.zeros((1, PAIR), F32)
    at = 0
    for i in range(blocks):
        k0, k1 = key_range(i)
        width = k1 - k0
        bias = bias_ref[at : at + width, :]
        at += width
        rows = slice(i * TILE, (i + 1) * TILE)
        q = q_ref[rows, :]
        g = g_ref[rows, :]
        keys = k_ref[k0:k1, :]
        values = v_ref[k0:k1, :]
        qm = head_masks(TILE)
        km = head_masks(width)
        qs, gs, ks, ps, ds = [], [], [], [], []
        for h in range(2):
            qh = only(qm[h], q)
            gh = only(qm[h], g)
            scores = nt(keys, qh) + bias
            p = jnp.exp(scores - lse_ref[0, h : h + 1, rows])
            pull = p * nt(values, gh)
            inner = jnp.sum(pull, axis=0, keepdims=True)
            qs.append(qh)
            gs.append(gh)
            ks.append(only(km[h], keys))
            ps.append(p.astype(BF16))
            ds.append((pull - p * inner).astype(BF16))
        q2 = jnp.concatenate(qs, axis=0)
        g2 = jnp.concatenate(gs, axis=0)
        va_ref[k0:k1, :] += nn(jnp.concatenate(ps, axis=1), g2)
        ka_ref[k0:k1, :] += nn(jnp.concatenate(ds, axis=1), q2)
        dq = tn(jnp.concatenate(ds, axis=0), jnp.concatenate(ks, axis=0)) * (HD**-0.5)
        dq = turn_back(dq, rows).astype(BF16)
        dq_ref[rows, :] = dq
        sums_q += jnp.sum(dq.astype(F32), axis=0, keepdims=True)
    bq_ref[...] = sums_q
    dk = turn_back(ka_ref[...], slice(None)).astype(BF16)
    dk_ref[...] = dk
    bk_ref[...] = jnp.sum(dk.astype(F32), axis=0, keepdims=True)
    dv = va_ref[...].astype(BF16)
    dv_ref[...] = dv
    bv_ref[...] = jnp.sum(dv.astype(F32), axis=0, keepdims=True)


def middle_kernel(
    x_ref, mix_ref, cot_ref, sg_ref, sb_ref, wo0_ref, wo1_ref, ob_ref, ng_ref, nb_ref,
    wu0_ref, wu1_ref, ub_ref, fg_ref, fb_ref, wd0_ref, wd1_ref, db_ref,
    out_ref, dmid_ref, dmidb_ref, dmix_ref, sub1_ref, n2_ref, sub2_ref, dhid_ref,
    gsg_ref, gsb_ref, gob_ref, gng_ref, gnb_ref, gub_ref, gfg_ref, gfb_ref, gdb_ref,
    act_ref, slope_ref,
):
    half = wo0_ref.shape[0]
    fhalf = wd0_ref.shape[0]
    ff = 2 * fhalf
    unit1, inv1 = unit_rows(mix_ref[...])
    sub1 = (unit1 * sg_ref[...] + sb_ref[...]).astype(BF16)
    sub1_ref[...] = sub1
    middle = (
        x_ref[...].astype(F32)
        + (nn(sub1[:, :half], wo0_ref[...]) + nn(sub1[:, half:], wo1_ref[...]))
        + ob_ref[...]
    )
    unit2, inv2 = unit_rows(middle)
    normed2 = (unit2 * ng_ref[...] + nb_ref[...]).astype(BF16)
    n2_ref[...] = normed2
    rows = normed2.shape[0]
    total = jnp.zeros((rows, 1), F32)
    square = jnp.zeros((rows, 1), F32)
    step = 512
    for at in range(0, ff, step):
        w_ref, off = (wu0_ref, at) if at < fhalf else (wu1_ref, at - fhalf)
        hidden = nn(normed2, w_ref[:, off : off + step]) + ub_ref[:, at : at + step]
        gate = 0.5 + 0.5 * lax.erf(hidden * (0.5**0.5))
        active = hidden * gate
        act_ref[:, at : at + step] = active
        slope_ref[:, at : at + step] = gate + hidden * (
            jnp.exp(hidden * hidden * -0.5) * (1.0 / math.sqrt(2.0 * math.pi))
        )
        total += jnp.sum(active, axis=-1, keepdims=True)
        square += jnp.sum(active * active, axis=-1, keepdims=True)
    center3 = total * (1.0 / ff)
    inv3 = lax.rsqrt(square * (1.0 / ff) - center3 * center3 + 1e-05)
    cot = cot_ref[...]
    final = middle + db_ref[...]
    t_sum = jnp.zeros((rows, 1), F32)
    t_unit = jnp.zeros((rows, 1), F32)

    def unit3(at):
        return (act_ref[:, at : at + step] - center3) * inv3

    def back2(at):
        w_ref, off = (wd0_ref, at) if at < fhalf else (wd1_ref, at - fhalf)
        return nt(cot, w_ref[off : off + step, :])

    scaled = []
    for at in range(0, ff, step):
        w_ref, off = (wd0_ref, at) if at < fhalf else (wd1_ref, at - fhalf)
        unit = unit3(at)
        act_ref[:, at : at + step] = unit
        sub2 = (unit * fg_ref[:, at : at + step] + fb_ref[:, at : at + step]).astype(BF16)
        sub2_ref[:, at : at + step] = sub2
        final += nn(sub2, w_ref[off : off + step, :])
        grad = back2(at)
        add_rows(gfg_ref.at[:, at : at + step], grad * unit)
        add_rows(gfb_ref.at[:, at : at + step], grad)
        t = grad * fg_ref[:, at : at + step]
        scaled.append(t)
        t_sum += jnp.sum(t, axis=-1, keepdims=True)
        t_unit += jnp.sum(t * unit, axis=-1, keepdims=True)
    out_ref[...] = final.astype(BF16)
    t_sum = t_sum * (1.0 / ff)
    t_unit = t_unit * (1.0 / ff)
    dn2 = jnp.zeros(middle.shape, F32)
    for n, at in enumerate(range(0, ff, step)):
        w_ref, off = (wu0_ref, at) if at < fhalf else (wu1_ref, at - fhalf)
        dact = inv3 * (scaled[n] - t_sum - act_ref[:, at : at + step] * t_unit)
        dhid = (dact * slope_ref[:, at : at + step]).astype(BF16)
        dhid_ref[:, at : at + step] = dhid
        add_rows(gub_ref.at[:, at : at + step], dhid.astype(F32))
        dn2 += nt(dhid, w_ref[:, off : off + step])
    cotf = cot.astype(F32)
    add_rows(gdb_ref, cotf)
    add_rows(gng_ref, dn2 * unit2)
    add_rows(gnb_ref, dn2)
    dmid = cotf + norm_back(dn2, unit2, inv2, ng_ref[...])
    dmid_ref[...] = dmid
    dmidb = dmid.astype(BF16)
    dmidb_ref[...] = dmidb
    add_rows(gob_ref, dmidb.astype(F32))
    ds1 = jnp.concatenate([nt(dmidb, wo0_ref[...]), nt(dmidb, wo1_ref[...])], axis=1)
    add_rows(gsg_ref, ds1 * unit1)
    add_rows(gsb_ref, ds1)
    dmix_ref[...] = norm_back(ds1, unit1, inv1, sg_ref[...]).astype(BF16)


def finish_kernel(
    x_ref, dmid_ref, dq_ref, dk_ref, dv_ref, gain_ref, own_ref, oth_ref, out_ref, gg_ref, gb_ref
):
    half = own_ref.shape[2]
    dn1 = None
    for j, d_ref in enumerate((dq_ref, dk_ref, dv_ref)):
        d = d_ref[...]
        part = nt(d[:, :half], own_ref[j]) + nt(d[:, half:], oth_ref[j])
        dn1 = part if dn1 is None else dn1 + part
    unit, inv = unit_rows(x_ref[...].astype(F32))
    add_rows(gg_ref, dn1 * unit)
    add_rows(gb_ref, dn1)
    out_ref[...] = dmid_ref[...] + norm_back(dn1, unit, inv, gain_ref[...])


def call(kernel, grid, ins, outs, scratch, flops, name):
    moved = sum(a.size * a.dtype.itemsize for a, _, _ in ins)
    moved += sum(math.prod(s) * jnp.dtype(d).itemsize for s, d, _, _ in outs)
    return pl.pallas_call(
        kernel,
        grid=(grid,),
        in_specs=[pl.BlockSpec(b, m) for _, b, m in ins],
        out_specs=[pl.BlockSpec(b, m) for _, _, b, m in outs],
        out_shape=[jax.ShapeDtypeStruct(s, d) for s, d, _, _ in outs],
        scratch_shapes=scratch,
        compiler_params=pltpu.CompilerParams(
            dimension_semantics=("arbitrary",), vmem_limit_bytes=VMEM_BYTES
        ),
        cost_estimate=pl.CostEstimate(flops=flops, bytes_accessed=moved, transcendentals=0),
        name=name,
    )(*[a for a, _, _ in ins])


def fixed(a):
    return (a, a.shape, lambda i, n=a.ndim: (0,) * n)


def tiled(a, tile):
    return (a, (tile, a.shape[1]), lambda i: (i, 0))


def columns(a):
    return (a, (a.shape[0], PAIR), lambda i: (0, i))


def local(
    inputs, segment_ids, cotangent, attn_norm_gain, attn_norm_bias, qkv_weight, qkv_bias,
    attn_sub_gain, attn_sub_bias, out_weight, out_bias, ffn_norm_gain, ffn_norm_bias,
    up_weight, up_bias, ffn_sub_gain, ffn_sub_bias, down_weight, down_bias,
):
    _, length, width = inputs.shape
    half = qkv_weight.shape[2]
    fhalf = up_weight.shape[1]
    ff = 2 * fhalf
    pairs = width // PAIR
    tiles = length // TILE
    swap = [(0, 1), (1, 0)]

    def trade(a):
        return lax.ppermute(a, "tensor", swap)

    x = inputs[0]
    cot = cotangent[0]
    qkv_other = trade(qkv_weight)
    split = jnp.concatenate(
        [qkv_bias.reshape(-1), attn_sub_gain, attn_sub_bias, up_bias, ffn_sub_gain, ffn_sub_bias]
    )
    split_other = trade(split)
    out_other = trade(out_weight)
    up_other = trade(up_weight)
    down_other = trade(down_weight)

    def joined(start, size):
        return jnp.concatenate([split[start : start + size], split_other[start : start + size]])[None]

    qb = jnp.concatenate(
        [split[: 3 * half].reshape(3, half), split_other[: 3 * half].reshape(3, half)], axis=1
    )
    sg = joined(3 * half, half)
    sb = joined(4 * half, half)
    ub = joined(5 * half, fhalf)
    fg = joined(5 * half + fhalf, fhalf)
    fb = joined(5 * half + 2 * fhalf, fhalf)

    segment = lax.dynamic_slice_in_dim(segment_ids, lax.axis_index("tensor"), 1, 0)[0]
    index = jnp.arange(length, dtype=jnp.int32)
    begins = jnp.concatenate([jnp.ones((1,), jnp.bool_), segment[1:] != segment[:-1]])
    place = index - lax.cummax(jnp.where(begins, index, 0))
    frequency = jnp.exp(
        jnp.arange(HD // 2).astype(F32) * (-2.0 * math.log(10000.0) / HD)
    )
    angle = place.astype(F32)[:, None] * frequency
    cosine, sine = jnp.cos(angle), jnp.sin(angle)
    cos = jnp.concatenate([cosine] * 4, axis=1)
    sin = jnp.concatenate([-sine, sine, -sine, sine], axis=1)
    scol = segment[:, None]
    srow = segment[None, :]

    row = lambda v: v[None]
    mm = 2 * length * width
    normed1, q, k, v = call(
        project_kernel,
        tiles,
        [tiled(x, TILE), fixed(row(attn_norm_gain)), fixed(row(attn_norm_bias)), fixed(qkv_weight),
         fixed(qkv_other), fixed(qb), tiled(cos, TILE), tiled(sin, TILE)],
        [((length, width), BF16, (TILE, width), lambda i: (i, 0))] * 4,
        [],
        3 * mm * width,
        "project",
    )
    spans = sum(b - a for a, b in map(key_range, range(tiles)))
    pair_out = lambda dtype: ((length, width), dtype, (length, PAIR), lambda i: (0, i))
    mixed, lse = call(
        attend_kernel,
        pairs,
        [columns(q), columns(k), columns(v), fixed(scol), fixed(srow)],
        [pair_out(F32), ((pairs, 8, length), F32, (1, 8, length), lambda i: (i, 0, 0))],
        [pltpu.VMEM((TILE, spans), F32)],
        8 * mm * spans // tiles,
        "attend",
    )
    tile_out = lambda w, dtype: ((length, w), dtype, (TILE, w), lambda i: (i, 0))
    vec_out = lambda w: ((1, w), F32, (1, w), lambda i: (0, 0))
    (
        outputs, dmid, dmidb, dmix, sub1, normed2, sub2, dhid,
        g_sg, g_sb, g_ob, g_ng, g_nb, g_ub, g_fg, g_fb, g_db,
    ) = call(
        middle_kernel,
        tiles,
        [tiled(x, TILE), tiled(mixed, TILE), tiled(cot, TILE), fixed(sg), fixed(sb), fixed(out_weight),
         fixed(out_other), fixed(row(out_bias)), fixed(row(ffn_norm_gain)), fixed(row(ffn_norm_bias)),
         fixed(up_weight), fixed(up_other), fixed(ub), fixed(fg), fixed(fb), fixed(down_weight),
         fixed(down_other), fixed(row(down_bias))],
        [tile_out(width, BF16), tile_out(width, F32), tile_out(width, BF16), tile_out(width, BF16),
         tile_out(width, BF16), tile_out(width, BF16), tile_out(ff, BF16), tile_out(ff, BF16),
         vec_out(width), vec_out(width), vec_out(width), vec_out(width), vec_out(width),
         vec_out(ff), vec_out(ff), vec_out(ff), vec_out(width)],
        [pltpu.VMEM((TILE, ff), F32), pltpu.VMEM((TILE, ff), F32)],
        2 * mm * (width + 2 * ff),
        "middle",
    )

    def both(left, right, left_side, axis):
        size = (left if left_side else right).shape[1] // 2

        def product(start):
            a = left[:, start : start + size] if left_side else left
            b = right if left_side else right[:, start : start + size]
            return tn(a, b)

        return (product(0) + trade(product(size).astype(BF16)).astype(F32)).astype(BF16)

    down_grad = both(sub2, cot, True, 0)
    up_grad = both(normed2, dhid, False, 1)
    out_grad = both(sub1, dmidb, True, 0)
    down_grad, up_grad, out_grad = lax.psum((down_grad, up_grad, out_grad), "dp")

    dq, dk, dv, g_bq, g_bk, g_bv = call(
        attend_back_kernel,
        pairs,
        [columns(q), columns(k), columns(v), columns(dmix),
         (lse, (1, 8, length), lambda i: (i, 0, 0)), fixed(scol), fixed(srow), fixed(cos), fixed(sin)],
        [pair_out(BF16)] * 3 + [((1, width), F32, (1, PAIR), lambda i: (0, i))] * 3,
        [pltpu.VMEM((spans, TILE), F32), pltpu.VMEM((length, PAIR), F32),
         pltpu.VMEM((length, PAIR), F32)],
        20 * mm * spans // tiles,
        "attend_back",
    )
    qkv_grad = jnp.stack([both(normed1, d, False, 1) for d in (dq, dk, dv)])
    input_grad, g_ag, g_ab = call(
        finish_kernel,
        tiles,
        [tiled(x, TILE), tiled(dmid, TILE), tiled(dq, TILE), tiled(dk, TILE), tiled(dv, TILE),
         fixed(row(attn_norm_gain)), fixed(qkv_weight), fixed(qkv_other)],
        [tile_out(width, F32), vec_out(width), vec_out(width)],
        [],
        3 * mm * width,
        "finish",
    )
    cut = [g_bq, g_bk, g_bv, g_sg, g_sb, g_ub, g_fg, g_fb]
    shared = [g_ag, g_ab, g_ob, g_ng, g_nb, g_db]
    mine = jnp.concatenate([c[0, : c.shape[1] // 2] for c in cut] + [s[0] for s in shared])
    theirs = jnp.concatenate([c[0, c.shape[1] // 2 :] for c in cut] + [s[0] for s in shared])
    small = mine + trade(theirs)
    rows = -(-small.size // half)
    pad = jnp.zeros((rows * half - small.size,), F32)
    small = jnp.concatenate([small, pad]).reshape(rows, half).astype(BF16)
    last = jnp.concatenate([qkv_grad.reshape(3 * width, half), small])
    last = lax.psum(last, "dp").astype(F32)
    qkv_grad = last[: 3 * width].reshape(3, width, half)
    small = last[3 * width :].reshape(-1)
    pieces = []
    at = 0
    for size in [c.shape[1] // 2 for c in cut] + [s.shape[1] for s in shared]:
        pieces.append(small[at : at + size])
        at += size
    g_bq, g_bk, g_bv, g_sg, g_sb, g_ub, g_fg, g_fb, g_ag, g_ab, g_ob, g_ng, g_nb, g_db = pieces
    return (
        outputs[None], input_grad[None], g_ag, g_ab, qkv_grad, jnp.stack([g_bq, g_bk, g_bv]),
        g_sg, g_sb, out_grad.astype(F32), g_ob, g_ng, g_nb, up_grad.astype(F32), g_ub, g_fg, g_fb,
        down_grad.astype(F32), g_db,
    )


def solution(mesh):
    rows = P(("dp", "tensor"), None, None)
    in_specs = (
        rows, P("dp", None), rows, P(), P(), P(None, None, "tensor"), P(None, "tensor"),
        P("tensor"), P("tensor"), P("tensor", None), P(), P(), P(), P(None, "tensor"),
        P("tensor"), P("tensor"), P("tensor"), P("tensor", None), P(),
    )
    out_specs = (
        rows, rows, P(), P(), P(None, None, "tensor"), P(None, "tensor"), P("tensor"), P("tensor"),
        P("tensor", None), P(), P(), P(), P(None, "tensor"), P("tensor"), P("tensor"), P("tensor"),
        P("tensor", None), P(),
    )
    return jax.shard_map(local, mesh=mesh, in_specs=in_specs, out_specs=out_specs, check_vma=False)
```

time: 1250 us -> 469 us (0.38)
  local copies, waits for them, and re-layouts: 292 us -> 25 us
  matrix products: 268 us -> 39.2 us
  other arithmetic: 177 us -> 18.3 us
  waiting for transfers between devices: 369 us -> 233 us
  Pallas kernels: 0 us -> 128 us
  blocking collectives: 97 us -> 0 us
  loops' own time: 17.1 us -> 0 us
    dot_general x40 -> x12, matrix products: 268 us -> 39.2 us  [tn(): lax.dot_general(a, b, (((0,), (0,)), ((), ())), preferred_element_type=F32)]
    dynamic_update_slice x14 -> x0, local copies, waits for them, and re-layouts: 142 us -> none  [local(): lax.map(forward_seq, (queries, key_rows, value_rows, segment_ids))]
    pallas_call x0 -> x5, Pallas kernels: none -> 128 us  [call(): pl.pallas_call(kernel, grid=(grid,), in_specs=[pl.BlockSpec(b, m) for _,...]
    psum x5 -> x0, blocking collectives: 97 us -> none  [the longest x1 82.5 us: local(): lax.psum((attn_norm_gain_grad, attn_norm_bias_grad, qkv_weight_grad, qkv_...]
    reduce_sum x15 -> x0, other arithmetic: 83 us -> none  [the longest x1 21.4 us: local(): up_bias_grad = jnp.sum(grad_hidden, axis=0, dtype=jnp.float32)]
    psum x2 -> x1, waiting for transfers between devices: 302 us -> 233 us  [local(): last = lax.psum(last, 'dp').astype(F32)]
    convert_element_type x8 -> x6, other arithmetic: 50.6 us -> 8.39 us  [the longest x1 2.82 us: local(): up_grad.astype(F32)]
    all_gather x4 -> x0, waiting for transfers between devices: 33.2 us -> none  [the longest x1 14.2 us: local(): lax.all_gather(grad_middle.astype(jnp.bfloat16), 'tensor', axis=0, tiled=...]
  transfers between devices with their start and end apart: 9 -> 13, of which waited for: 7 -> 1; matrix products, arithmetic and copies ran while one was open for 8% -> 10% of each run, Pallas kernels for 0% -> 15%
where the time goes in v1:
time: 469 us; the launch traced here: 461 us
  waiting for transfers between devices  233 us (50%)
  Pallas kernels  128 us (27%)
  matrix products  39.2 us (8%)
  local copies, waits for them, and re-layouts  25 us (5%)
  other arithmetic  18.3 us (4%)
  between operations  15.4 us (3%)
    psum x1, waiting for transfers between devices, local(): last = lax.psum(last, 'dp').astype(F32)  233 us
    pallas_call x5, Pallas kernels, call(): pl.pallas_call(kernel, grid=(grid,), in_specs=[pl.BlockSpec(b, m) for _,...  128 us
    dot_general x12, matrix products, tn(): lax.dot_general(a, b, (((0,), (0,)), ((), ())), preferred_element_type=F32)  39.2 us
  transfers between devices with their start and end apart: 13, of which 1 were waited for; matrix products, arithmetic and copies ran while one was open for 10% of the time, Pallas kernels for 15%

profile of v1, /device:TPU:0, one launch (start us, length us, event | category | flops | bytes accessed | tf_op | source)
XLA Modules:
  0.0 461.4 jit_solution(14764290654194354542)
XLA Ops:
  7.2 0.7 reshape.112
  8.0 0.7 constant_dynamic-update-slice_fusion.12
  8.6 0.7 constant_dynamic-update-slice_fusion.9
  9.3 0.7 constant_dynamic-update-slice_fusion.6
  10.0 0.7 constant_dynamic-update-slice_fusion.3
  10.7 0.7 constant_dynamic-update-slice_fusion
  13.0 0.7 fusion.37
  13.7 0.9 compare_reduce_fusion
  15.2 1.9 fusion.19
  17.3 1.9 pad_maximum_fusion.2
  19.1 0.6 constant_dynamic-slice_fusion.srow_ref
  19.7 0.6 broadcast_in_dim.46.gain_ref
  20.3 0.6 broadcast_in_dim.47.bias_ref
  20.9 1.0 copy.40.scol_ref
  21.9 0.6 broadcast_in_dim.51.ob_ref
  22.5 0.6 broadcast_in_dim.52.ng_ref
  23.1 0.6 broadcast_in_dim.53.nb_ref
  23.7 0.6 broadcast_in_dim.57.db_ref
  24.3 0.6 broadcast_in_dim.49.sg_ref
  24.9 0.6 broadcast_in_dim.50.sb_ref
  25.5 0.6 pad_maximum_fusion.4.qb_ref
  26.1 0.6 pad_maximum_fusion.7
  26.7 0.6 pad_maximum_fusion.5
  27.3 9.4 %project.1 = (bf16[1024,768]{1,0:T(8,128)(2,1)}, bf16[1024,768]{1,0:T(8,128)(2,1)}, bf16[1024,768]{1,0:T(8,128)(2,1)}, bf16[1024,768]{1,0:T(8,128)(2,1)}) custom-call(bf16[1024,768]{1,0:T(8,128)(2,1)} %bitcast.44, f32[1,768]{1,0:T(1,128)} %broadcast_in_dim.46.gain_ref, f32[1,768]{1,0:T(1,128)} %broadcast_in_dim.47.bias_ref, bf16[3,768,384]{2,1,0:T(8,128)(2,1)} %own_ref.3, ...), custom_call_target="tpu_custom_call" | custom-call | flops 3623878656 | bytes 12467200 | tf_op jit(solution)/shard_map/project/pallas_call | solution.py:326
  36.7 20.4 %attend.1 = (f32[1024,768]{1,0:T(8,128)}, f32[6,8,1024]{2,1,0:T(8,128)}) custom-call(bf16[1024,768]{1,0:T(8,128)(2,1)} %get-tuple-element.50.q_ref, bf16[1024,768]{1,0:T(8,128)(2,1)} %get-tuple-element.51.k_ref, bf16[1024,768]{1,0:T(8,128)(2,1)} %get-tuple-element.52.v_ref, s32[1024,1]{1,0:T(8,128)} %copy.40.scol_ref, ...), custom_call_target="tpu_custom_call" | custom-call | flops 7247757312 | bytes 8069120 | tf_op jit(solution)/shard_map/attend/pallas_call | solution.py:326
  57.1 0.8 copy-done.31
  57.9 0.8 copy-done.29
  58.6 60.3 %middle.1 = (bf16[1024,768]{1,0:T(8,128)(2,1)}, f32[1024,768]{1,0:T(8,128)}, bf16[1024,768]{1,0:T(8,128)(2,1)}, bf16[1024,768]{1,0:T(8,128)(2,1)}, bf16[1024,768...) custom-call(bf16[1024,768]{1,0:T(8,128)(2,1)} %bitcast.45, ...), custom_call_target="tpu_custom_call" | custom-call | flops 21743271936 | bytes 40611840 | tf_op jit(solution)/shard_map/middle/pallas_call | solution.py:326
  119.0 6.6 %convolution_convert_fusion = bf16[1536,768]{1,0:T(8,128)(2,1)} fusion(bf16[1024,3072]{1,0:T(8,128)(2,1)} %get-tuple-element.81, bf16[1,1024,768]{2,1,0:T(8,128)(2,1)} %param.21), kind=kOutput, calls=%fused_computation.2 | convolution fusion | flops 2417098752 | bytes 7077888 | tf_op jit(solution)/shard_map/dot_general | solution.py:28
  125.6 4.0 convolution_convert_fusion.1
  130.1 26.0 %attend_back.1 = (bf16[1024,768]{1,0:T(8,128)(2,1)}, bf16[1024,768]{1,0:T(8,128)(2,1)}, bf16[1024,768]{1,0:T(8,128)(2,1)}, f32[1,768]{1,0:T(1,128)}, f32[1,768]{1,0:T(1,128)}, /*index=5*/f32[1,768]{1,0:T(1,128)}) custom-call(bf16[1024,768]{1,0:T(8,128)(2,1)} %get-tuple-element.50.q_ref, bf16[1024,768]{1,0:T(8,128)(2,1)} %get-tuple-element.51.k_ref, ...), custom_call_target="tpu_custom_call" | custom-call | flops 18119393280 | bytes 12272640 | tf_op jit(solution)/shard_map/attend_back/pallas_call | solution.py:326
  156.1 3.6 convolution_convert_fusion.5
  159.7 1.8 convolution_convert_fusion.4
  161.6 1.0 convolution_convert_fusion.3
  163.0 11.5 %finish.1 = (f32[1024,768]{1,0:T(8,128)}, f32[1,768]{1,0:T(1,128)}, f32[1,768]{1,0:T(1,128)}) custom-call(bf16[1024,768]{1,0:T(8,128)(2,1)} %bitcast.46, f32[1024,768]{1,0:T(8,128)} %get-tuple-element.55.dmid_ref, bf16[1024,768]{1,0:T(8,128)(2,1)} %get-tuple-element.58.dq_ref, bf16[1024,768]{1,0:T(8,128)(2,1)} %get-tuple-element.59.dk_ref, ...), custom_call_target="tpu_custom_call" | custom-call | flops 3623878656 | bytes 16131072 | tf_op jit(solution)/shard_map/finish/pallas_call | solution.py:326
  174.5 0.7 reduce.10
  175.2 0.7 reduce.11
  176.9 3.3 convolution_convert_fusion.2
  180.8 2.9 fusion.10
  183.8 2.2 fusion.9
  186.1 1.0 fusion.8
  187.4 1.3 copy-done.36
  189.2 2.7 fusion.7
  191.9 1.4 pad_maximum_fusion
  193.3 0.6 copy-done.30
  193.9 6.1 %add_convert_fusion = bf16[1536,768]{1,0:T(8,128)(2,1)} fusion(bf16[1536,768]{1,0:T(8,128)(2,1)} %collective-permute-done.11, bf16[1024,3072]{1,0:T(8,128)(2,1)S(1)} %bitcast.53, bf16[1,1024,768]{2,1,0:T(8,128)(2,1)S(1)} %copy-done.30), kind=kOutput, calls=%fused_computation | convolution fusion | flops 2419458048 | bytes 9437184 | tf_op jit(solution)/shard_map/dot_general | solution.py:28
  200.0 4.1 add_convert_fusion.1
  204.1 232.7 %all-reduce.3.cloned.1.call-done = (bf16[2333,384]{1,0:T(8,128)(2,1)}, bf16[384,768]{1,0:T(8,128)(2,1)}, bf16[768,1536]{1,0:T(8,128)(2,1)}, bf16[1536,768]{1,0:T(8,128)(2,1)}) async-done(((bf16[2333,384]{1,0:T(8,128)(2,1)}, bf16[384,768]{1,0:T(8,128)(2,1)}, bf16[768,1536]{1,0:T(8,128)(2,1)}, bf16[1536,768]{1,0:T(8,128)(2,1)}), (bf16[2333,384]{1,0:T(8,128)(2,1)}, bf16[384,768]{1,0:T(8,128)(2,1)}, ...) | async-done | bytes 7100176 | tf_op jit(solution)/shard_map/psum | solution.py:496
  436.8 1.8 convert_element_type.99
  438.8 2.0 slice.292
  440.8 0.6 slice.293
  441.6 2.8 convert_element_type.107
  444.5 2.5 convert_element_type.111
  447.0 0.6 slice_reduce_fusion.7
  447.6 1.1 convert_element_type.103
  448.7 0.6 slice.274
  449.3 0.6 slice.276
  449.9 0.6 slice.278
  450.5 0.6 slice.254
  451.1 0.6 slice.256
  451.7 0.6 slice.266
  452.3 0.6 slice.268
  452.9 0.6 slice.270
  453.5 0.6 slice.282
  (173 shorter events, 5.7 us)
Async XLA Ops:
  7.2 429.6 %all-reduce.3.cloned.1.call-start = ((), (), s32[]{:S(2)}) async-start(), calls=%async_computation | async-start | bytes 14204928 | tf_op jit(solution)/shard_map/psum | solution.py:496
  11.4 12.8 %collective-permute-start.1 = (f32[6528]{0:T(1024)S(1)}, f32[6528]{0:T(1024)S(1)}, u32[]{:S(2)}, u32[]{:S(2)}) collective-permute-start(f32[6528]{0:T(1024)S(1)} %constant_dynamic-update-slice_fusion), channel_id=1, source_target_pairs={{0,1},{1,0},{2,3},{3,2},{4,5},{5,4},{6,7},{7,6},{8,9},{9,8},{10,11... | collective-permute-start | bytes 78344 | tf_op jit(solution)/shard_map/ppermute | solution.py:367
  11.9 15.4 %collective-permute-start = (bf16[3,768,384]{2,1,0:T(8,128)(2,1)}, bf16[3,768,384]{2,1,0:T(8,128)(2,1)}, u32[]{:S(2)}, u32[]{:S(2)}) collective-permute-start(bf16[3,768,384]{2,1,0:T(8,128)(2,1)} %own_ref.3), channel_id=1, source_target_pairs={{0,1},{1,0},{2,3},{3,2},{4,5},{5,4},{6,7},{7,6},{8,9},{9,8},{10,11... | collective-permute-start | bytes 5308424 | tf_op jit(solution)/shard_map/ppermute | solution.py:367
  12.0 45.1 %collective-permute-start.3 = (bf16[768,1536]{1,0:T(8,128)(2,1)}, bf16[768,1536]{1,0:T(8,128)(2,1)S(1)}, u32[]{:S(2)}, u32[]{:S(2)}) collective-permute-start(bf16[768,1536]{1,0:T(8,128)(2,1)} %wu0_ref.1), channel_id=1, source_target_pairs={{0,1},{1,0},{2,3},{3,2},{4,5},{5,4},{6,7},{7,6},{8,9},{9,8},{10,11... | collective-permute-start | bytes 7077896 | tf_op jit(solution)/shard_map/ppermute | solution.py:367
  12.4 44.6 %collective-permute-start.4 = (bf16[1536,768]{1,0:T(8,128)(2,1)}, bf16[1536,768]{1,0:T(8,128)(2,1)}, u32[]{:S(2)}, u32[]{:S(2)}) collective-permute-start(bf16[1536,768]{1,0:T(8,128)(2,1)} %wd0_ref.1), channel_id=1, source_target_pairs={{0,1},{1,0},{2,3},{3,2},{4,5},{5,4},{6,7},{7,6},{8,9},{9,8},{10,11... | collective-permute-start | bytes 7077896 | tf_op jit(solution)/shard_map/ppermute | solution.py:367
  12.5 44.6 %collective-permute-start.2 = (bf16[384,768]{1,0:T(8,128)(2,1)}, bf16[384,768]{1,0:T(8,128)(2,1)S(1)}, u32[]{:S(2)}, u32[]{:S(2)}) collective-permute-start(bf16[384,768]{1,0:T(8,128)(2,1)} %wo0_ref.1), channel_id=1, source_target_pairs={{0,1},{1,0},{2,3},{3,2},{4,5},{5,4},{6,7},{7,6},{8,9},{9,8},{10,11... | collective-permute-start | bytes 1769480 | tf_op jit(solution)/shard_map/ppermute | solution.py:367
  17.1 2.0 copy-start.7
  17.1 2.6 copy-start.14
  17.1 3.2 copy-start.15
  17.1 4.8 %copy-start.16 = (f32[768]{0:T(1024)S(1)}, f32[768]{0:T(1024)}, u32[]{:S(2)}) copy-start(f32[768]{0:T(1024)} %param.29) | copy-start | bytes 9220
  17.2 5.3 %copy-start.17 = (f32[768]{0:T(1024)S(1)}, f32[768]{0:T(1024)}, u32[]{:S(2)}) copy-start(f32[768]{0:T(1024)} %param.30) | copy-start | bytes 9220
  17.2 5.9 %copy-start.18 = (f32[768]{0:T(1024)S(1)}, f32[768]{0:T(1024)}, u32[]{:S(2)}) copy-start(f32[768]{0:T(1024)} %param.31) | copy-start | bytes 9220
  17.2 6.5 %copy-start.19 = (f32[768]{0:T(1024)S(1)}, f32[768]{0:T(1024)}, u32[]{:S(2)}) copy-start(f32[768]{0:T(1024)} %param.37) | copy-start | bytes 9220
  17.2 7.1 %copy-start.12 = (f32[384]{0:T(512)S(1)}, f32[384]{0:T(512)}, u32[]{:S(2)}) copy-start(f32[384]{0:T(512)} %param.26) | copy-start | bytes 4612
  17.2 7.1 %copy-start.13 = (f32[384]{0:T(512)S(1)}, f32[384]{0:T(512)}, u32[]{:S(2)}) copy-start(f32[384]{0:T(512)} %param.27) | copy-start | bytes 4612
  17.2 8.3 %copy-start.8 = (f32[3,384]{1,0:T(4,128)S(1)}, f32[3,384]{1,0:T(4,128)}, u32[]{:S(2)}) copy-start(f32[3,384]{1,0:T(4,128)} %param.25) | copy-start | bytes 13828
  17.2 8.9 %copy-start.4 = (f32[1536]{0:T(1024)S(1)}, f32[1536]{0:T(1024)}, u32[]{:S(2)}) copy-start(f32[1536]{0:T(1024)} %param.35) | copy-start | bytes 18436
  17.2 9.5 %copy-start.5 = (f32[1536]{0:T(1024)S(1)}, f32[1536]{0:T(1024)}, u32[]{:S(2)}) copy-start(f32[1536]{0:T(1024)} %param.33) | copy-start | bytes 18436
  17.3 9.4 %copy-start.6 = (f32[1536]{0:T(1024)S(1)}, f32[1536]{0:T(1024)}, u32[]{:S(2)}) copy-start(f32[1536]{0:T(1024)} %param.34) | copy-start | bytes 18436
  57.0 0.8 copy-start.31
  57.1 1.6 copy-start.29
  119.0 6.6 %copy-start.40 = (bf16[1024,3072]{1,0:T(8,128)(2,1)S(1)}, bf16[1024,3072]{1,0:T(8,128)(2,1)}, u32[]{:S(2)}) copy-start(bf16[1024,3072]{1,0:T(8,128)(2,1)} %get-tuple-element.80) | copy-start | bytes 18874372
  119.0 6.6 %copy-start.41 = (bf16[1024,768]{1,0:T(8,128)(2,1)S(1)}, bf16[1024,768]{1,0:T(8,128)(2,1)}, u32[]{:S(2)}) copy-start(bf16[1024,768]{1,0:T(8,128)(2,1)} %get-tuple-element.79) | copy-start | bytes 4718596
  125.6 67.7 %collective-permute-start.11 = (bf16[1536,768]{1,0:T(8,128)(2,1)}, bf16[1536,768]{1,0:T(8,128)(2,1)}, u32[]{:S(2)}, u32[]{:S(2)}) collective-permute-start(bf16[1536,768]{1,0:T(8,128)(2,1)} %convolution_convert_fusion), channel_id=1, source_target_pairs={{0,1},{1,0},{2,3},{3,2},{4,5},{5,4},{6,7},{7,6},{8,9},{9,8},{10,11... | collective-permute-start | bytes 7077896 | tf_op jit(solution)/shard_map/ppermute | solution.py:367
  129.6 70.4 %collective-permute-start.10 = (bf16[768,1536]{1,0:T(8,128)(2,1)}, bf16[768,1536]{1,0:T(8,128)(2,1)S(1)}, u32[]{:S(2)}, u32[]{:S(2)}) collective-permute-start(bf16[768,1536]{1,0:T(8,128)(2,1)} %convolution_convert_fusion.1), channel_id=1, source_target_pairs={{0,1},{1,0},{2,3},{3,2},{4,5},{5,4},{6,7},{7,6},{8,9},{9,8},{10,11... | collective-permute-start | bytes 7077896 | tf_op jit(solution)/shard_map/ppermute | solution.py:367
  156.1 3.6 copy-start.34
  156.1 3.6 copy-start.38
  159.7 21.1 %collective-permute-start.5 = (bf16[768,384]{1,0:T(8,128)(2,1)}, bf16[768,384]{1,0:T(8,128)(2,1)}, u32[]{:S(2)}, u32[]{:S(2)}) collective-permute-start(bf16[768,384]{1,0:T(8,128)(2,1)} %convolution_convert_fusion.5), channel_id=1, source_target_pairs={{0,1},{1,0},{2,3},{3,2},{4,5},{5,4},{6,7},{7,6},{8,9},{9,8},{10,11... | collective-permute-start | bytes 1769480 | tf_op jit(solution)/shard_map/ppermute | solution.py:367
  159.7 1.8 copy-start.32
  161.5 1.1 copy-start.24
  161.5 1.1 copy-start.23
  161.5 1.1 copy-start.22
  161.5 1.2 copy-start.21
  161.5 1.2 copy-start.20
  161.6 1.2 copy-start.11
  161.6 1.2 copy-start.10
  161.6 1.3 copy-start.9
  162.9 13.0 %copy-start.28 = (f32[1,768]{1,0:T(1,128)S(1)}, f32[1,768]{1,0:T(1,128)}, u32[]{:S(2)}) copy-start(f32[1,768]{1,0:T(1,128)} %get-tuple-element.73) | copy-start | bytes 9220
  162.9 13.0 %copy-start.27 = (f32[1,768]{1,0:T(1,128)S(1)}, f32[1,768]{1,0:T(1,128)}, u32[]{:S(2)}) copy-start(f32[1,768]{1,0:T(1,128)} %get-tuple-element.74) | copy-start | bytes 9220
  162.9 13.0 %copy-start.26 = (f32[1,768]{1,0:T(1,128)S(1)}, f32[1,768]{1,0:T(1,128)}, u32[]{:S(2)}) copy-start(f32[1,768]{1,0:T(1,128)} %get-tuple-element.75) | copy-start | bytes 9220
  162.9 13.1 %copy-start.25 = (f32[1,768]{1,0:T(1,128)S(1)}, f32[1,768]{1,0:T(1,128)}, u32[]{:S(2)}) copy-start(f32[1,768]{1,0:T(1,128)} %get-tuple-element.76) | copy-start | bytes 9220
  176.3 3.9 collective-permute-start.8
  180.2 7.2 %collective-permute-start.9 = (bf16[384,768]{1,0:T(8,128)(2,1)}, bf16[384,768]{1,0:T(8,128)(2,1)}, u32[]{:S(2)}, u32[]{:S(2)}) collective-permute-start(bf16[384,768]{1,0:T(8,128)(2,1)} %convolution_convert_fusion.2), channel_id=1, source_target_pairs={{0,1},{1,0},{2,3},{3,2},{4,5},{5,4},{6,7},{7,6},{8,9},{9,8},{10,11... | collective-permute-start | bytes 1769480 | tf_op jit(solution)/shard_map/ppermute | solution.py:367
  180.2 3.6 collective-permute-start.6
  180.7 3.1 copy-start.35
  180.7 3.1 copy-start.39
  180.7 5.3 %collective-permute-start.7 = (bf16[768,384]{1,0:T(8,128)(2,1)S(1)}, bf16[768,384]{1,0:T(8,128)(2,1)S(1)}, u32[]{:S(2)}, u32[]{:S(2)}) collective-permute-start(bf16[768,384]{1,0:T(8,128)(2,1)S(1)} %convolution_convert_fusion.3), channel_id=1, source_target_pairs={{0,1},{1,0},{2,3},{3,2},{4,5},{5,4},{6,7},{7,6},{8,9},{9,8},{10,11... | collective-permute-start | bytes 1769480 | tf_op jit(solution)/shard_map/ppermute | solution.py:367
  183.8 2.3 copy-start.33
  186.0 7.3 %slice-start.2 = ((s8[6291456]{0:T(1024)(128)(4,1)}), s8[4194304]{0:T(1024)(128)(4,1)S(1)}, s32[]{:S(2)}) async-start(s8[6291456]{0:T(1024)(128)(4,1)} %bitcast.52), calls=%async_computation.3 | async-start | bytes 8388608
  187.1 1.6 copy-start.36
  187.1 2.1 copy-start.37
  187.1 6.2 %slice-start.3 = ((s8[6291456]{0:T(1024)(128)(4,1)}), s8[2097152]{0:T(1024)(128)(4,1)S(1)}, s32[]{:S(2)}) async-start(s8[6291456]{0:T(1024)(128)(4,1)} %bitcast.52), calls=%async_computation.4 | async-start | bytes 4194304
  191.9 2.1 copy-start.30
  191.9 8.1 %slice-start = ((s8[6291456]{0:T(1024)(128)(4,1)}), s8[4194304]{0:T(1024)(128)(4,1)S(1)}, s32[]{:S(2)}) async-start(s8[6291456]{0:T(1024)(128)(4,1)} %bitcast.50), calls=%async_computation.1 | async-start | bytes 8388608
  193.3 6.7 %slice-start.1 = ((s8[6291456]{0:T(1024)(128)(4,1)}), s8[2097152]{0:T(1024)(128)(4,1)S(1)}, s32[]{:S(2)}) async-start(s8[6291456]{0:T(1024)(128)(4,1)} %bitcast.50), calls=%async_computation.2 | async-start | bytes 4194304
  193.3 6.7 %copy-start.42 = (bf16[1024,768]{1,0:T(8,128)(2,1)S(1)}, bf16[1024,768]{1,0:T(8,128)(2,1)}, u32[]{:S(2)}) copy-start(bf16[1024,768]{1,0:T(8,128)(2,1)} %get-tuple-element.79) | copy-start | bytes 4718596
  436.8 2.0 copy-start
  438.8 2.8 copy-start.2
  441.6 2.8 copy-start.1
  444.5 3.1 copy-start.3
Sparse Core Ops, SparseCore 0:
  204.2 232.4 all-reduce.2

commit v2 on v1

--- a/solution.py
+++ b/solution.py
@@ -1,3 +1,4 @@
+import functools
 import math
 
 import jax
@@ -350,7 +351,126 @@
     return (a, (a.shape[0], PAIR), lambda i: (0, i))
 
 
+def bit_order(count, stream):
+    bits = list(range(count.bit_length() - 1))
+    turn = min(3, len(bits))
+    return bits[stream % turn : turn] + bits[: stream % turn] + bits[turn:]
+
+
+def dp_sum_kernel(count, plan, *refs):
+    arrays = max(p[0] for p in plan) + 1
+    ins = refs[:arrays]
+    outs = refs[arrays : 2 * arrays]
+    parts = refs[2 * arrays : 3 * arrays]
+    send_sem, recv_sem = refs[3 * arrays :]
+    levels = count.bit_length() - 1
+    me = lax.axis_index("dp")
+    bit_of = lambda bit: (me // (1 << bit)) % 2
+    peer = lambda bit: me + (1 - 2 * bit_of(bit)) * (1 << bit)
+    barrier = pltpu.get_barrier_semaphore()
+    for bit in range(levels):
+        pl.semaphore_signal(
+            barrier, inc=1, device_id={"dp": peer(bit)}, device_id_type=pl.DeviceIdType.MESH
+        )
+    pl.semaphore_wait(barrier, levels)
+
+    def copy(src, dst, chain, step, bit):
+        return pltpu.make_async_remote_copy(
+            src_ref=src, dst_ref=dst, send_sem=send_sem.at[chain, step],
+            recv_sem=recv_sem.at[chain, step], device_id={"dp": peer(bit)},
+            device_id_type=pl.DeviceIdType.MESH,
+        )
+
+    size_at = [count >> (s + 1) for s in range(levels)]
+    base_at = [count - (count >> s) for s in range(levels)]
+    sent = []
+
+    def halve(chain, step):
+        a, stream, c0, c1 = plan[chain]
+        bit = bit_order(count, stream)[step]
+        size = size_at[step]
+        away = (1 - bit_of(bit)) * size
+        if step == 0:
+            src = ins[a].at[pl.ds(away, size), :, c0:c1]
+        else:
+            src = parts[a].at[pl.ds(base_at[step - 1] + away, size), :, c0:c1]
+        dst = parts[a].at[pl.ds(base_at[step], size), :, c0:c1]
+        c = copy(src, dst, chain, step, bit)
+        c.start()
+        sent.append(c)
+        return c
+
+    starts = {}
+
+    def double(chain, step):
+        a, stream, c0, c1 = plan[chain]
+        order = bit_order(count, stream)
+        level = levels - 1 - step
+        first = sum(bit_of(order[s]) * size_at[s] for s in range(level + 1))
+        view = outs[a].at[pl.ds(first, size_at[level]), :, c0:c1]
+        c = copy(view, view, chain, levels + step, order[level])
+        c.start()
+        sent.append(c)
+        return c
+
+    chains = range(len(plan))
+    flying = {chain: halve(chain, 0) for chain in chains}
+    for step in range(levels):
+        for chain in chains:
+            a, stream, c0, c1 = plan[chain]
+            order = bit_order(count, stream)
+            flying[chain].wait_recv()
+            kept = bit_of(order[step]) * size_at[step]
+            base = base_at[step]
+
+            def total(i):
+                own = (
+                    ins[a][kept + i, :, c0:c1]
+                    if step == 0
+                    else parts[a][base_at[step - 1] + kept + i, :, c0:c1]
+                )
+                return (own.astype(F32) + parts[a][base + i, :, c0:c1].astype(F32)).astype(BF16)
+
+            if step < levels - 1:
+
+                def add(i, carry):
+                    parts[a][base + i, :, c0:c1] = total(i)
+                    return carry
+
+                lax.fori_loop(0, size_at[step], add, 0)
+                flying[chain] = halve(chain, step + 1)
+            else:
+                mine = sum(bit_of(order[s]) * size_at[s] for s in range(levels))
+                outs[a][mine, :, c0:c1] = total(0)
+                flying[chain] = double(chain, 0)
+    for step in range(levels):
+        for chain in chains:
+            flying[chain].wait_recv()
+            if step < levels - 1:
+                flying[chain] = double(chain, step + 1)
+    for c in sent:
+        c.wait_send()
+
+
+def dp_sum(count, arrays, plan):
+    vmem = pl.BlockSpec(memory_space=pltpu.VMEM)
+    levels = count.bit_length() - 1
+    return pl.pallas_call(
+        functools.partial(dp_sum_kernel, count, plan),
+        in_specs=[vmem] * len(arrays),
+        out_specs=[vmem] * len(arrays),
+        out_shape=[jax.ShapeDtypeStruct(a.shape, a.dtype) for a in arrays],
+        scratch_shapes=[pltpu.VMEM(a.shape, a.dtype) for a in arrays]
+        + [pltpu.SemaphoreType.DMA((len(plan), 2 * levels))] * 2,
+        compiler_params=pltpu.CompilerParams(
+            collective_id=0, has_side_effects=True, vmem_limit_bytes=VMEM_BYTES
+        ),
+        name="dp_sum",
+    )(*arrays)
+
+
 def local(
+    count,
     inputs, segment_ids, cotangent, attn_norm_gain, attn_norm_bias, qkv_weight, qkv_bias,
     attn_sub_gain, attn_sub_bias, out_weight, out_bias, ffn_norm_gain, ffn_norm_bias,
     up_weight, up_bias, ffn_sub_gain, ffn_sub_bias, down_weight, down_bias,
@@ -447,7 +567,7 @@
         "middle",
     )
 
-    def both(left, right, left_side, axis):
+    def merged(left, right, left_side):
         size = (left if left_side else right).shape[1] // 2
 
         def product(start):
@@ -457,11 +577,9 @@
 
         return (product(0) + trade(product(size).astype(BF16)).astype(F32)).astype(BF16)
 
-    down_grad = both(sub2, cot, True, 0)
-    up_grad = both(normed2, dhid, False, 1)
-    out_grad = both(sub1, dmidb, True, 0)
-    down_grad, up_grad, out_grad = lax.psum((down_grad, up_grad, out_grad), "dp")
-
+    down_grad = merged(sub2, cot, True)
+    up_grad = merged(normed2, dhid, False)
+    out_grad = merged(sub1, dmidb, True)
     dq, dk, dv, g_bq, g_bk, g_bv = call(
         attend_back_kernel,
         pairs,
@@ -473,7 +591,7 @@
         20 * mm * spans // tiles,
         "attend_back",
     )
-    qkv_grad = jnp.stack([both(normed1, d, False, 1) for d in (dq, dk, dv)])
+    qkv_grad = [merged(normed1, d, False) for d in (dq, dk, dv)]
     input_grad, g_ag, g_ab = call(
         finish_kernel,
         tiles,
@@ -489,13 +607,25 @@
     mine = jnp.concatenate([c[0, : c.shape[1] // 2] for c in cut] + [s[0] for s in shared])
     theirs = jnp.concatenate([c[0, c.shape[1] // 2 :] for c in cut] + [s[0] for s in shared])
     small = mine + trade(theirs)
-    rows = -(-small.size // half)
-    pad = jnp.zeros((rows * half - small.size,), F32)
-    small = jnp.concatenate([small, pad]).reshape(rows, half).astype(BF16)
-    last = jnp.concatenate([qkv_grad.reshape(3 * width, half), small])
-    last = lax.psum(last, "dp").astype(F32)
-    qkv_grad = last[: 3 * width].reshape(3, width, half)
-    small = last[3 * width :].reshape(-1)
+    pad = jnp.zeros((-small.size % (16 * PAIR * count),), F32)
+    small = jnp.concatenate([small, pad]).astype(BF16).reshape(count, -1, PAIR)
+    out_grad = jnp.concatenate([out_grad[:, :half], out_grad[:, half:]])
+    wide = jnp.concatenate(qkv_grad + [out_grad], axis=1)
+    blocks = lambda a: a.reshape(count, a.shape[0] // count, a.shape[1])
+    plan = []
+    for part in range(2):
+        for n, c in enumerate((width, 2 * width, 4 * half)):
+            plan.append((n, n, part * c // 2, (part + 1) * c // 2))
+    plan.append((3, 2, 0, PAIR))
+    down_grad, up_grad, wide, small = dp_sum(
+        count, [blocks(down_grad), blocks(up_grad), blocks(wide), small], plan
+    )
+    down_grad = down_grad.reshape(fhalf, width)
+    up_grad = up_grad.reshape(width, fhalf)
+    wide = wide.reshape(width, 4 * half).astype(F32)
+    qkv_grad = jnp.stack([wide[:, j * half : (j + 1) * half] for j in range(3)])
+    out_grad = jnp.concatenate([wide[:half, 3 * half :], wide[half:, 3 * half :]], axis=1)
+    small = small.reshape(-1).astype(F32)
     pieces = []
     at = 0
     for size in [c.shape[1] // 2 for c in cut] + [s.shape[1] for s in shared]:
@@ -504,7 +634,7 @@
     g_bq, g_bk, g_bv, g_sg, g_sb, g_ub, g_fg, g_fb, g_ag, g_ab, g_ob, g_ng, g_nb, g_db = pieces
     return (
         outputs[None], input_grad[None], g_ag, g_ab, qkv_grad, jnp.stack([g_bq, g_bk, g_bv]),
-        g_sg, g_sb, out_grad.astype(F32), g_ob, g_ng, g_nb, up_grad.astype(F32), g_ub, g_fg, g_fb,
+        g_sg, g_sb, out_grad, g_ob, g_ng, g_nb, up_grad.astype(F32), g_ub, g_fg, g_fb,
         down_grad.astype(F32), g_db,
     )
 
@@ -521,4 +651,5 @@
         P("tensor", None), P(), P(), P(), P(None, "tensor"), P("tensor"), P("tensor"), P("tensor"),
         P("tensor", None), P(),
     )
-    return jax.shard_map(local, mesh=mesh, in_specs=in_specs, out_specs=out_specs, check_vma=False)
+    body = functools.partial(local, mesh.shape["dp"])
+    return jax.shard_map(body, mesh=mesh, in_specs=in_specs, out_specs=out_specs, check_vma=False)

time: 469 us -> 364 us (0.78)
  waiting for transfers between devices: 233 us -> 0.05 us
  Pallas kernels: 128 us -> 266 us
  between operations: 15.4 us -> 2 us
  other arithmetic: 18.3 us -> 27.7 us
    psum x1 -> x0, waiting for transfers between devices: 233 us -> none  [local(): last = lax.psum(last, 'dp').astype(F32)]
    pallas_call x0 -> x1, Pallas kernels: none -> 138 us  [dp_sum(): pl.pallas_call(functools.partial(dp_sum_kernel, count, plan), in_specs=[v...]
    concatenate x1 -> x2, other arithmetic: 1.41 us -> 8.72 us  [the longest x1 7.62 us: local(): wide = jnp.concatenate(qkv_grad + [out_grad], axis=1)]
    slice x13 -> x3, local copies, waits for them, and re-layouts: 6.63 us -> 1.81 us  [local(): pieces.append(small[at:at + size])]
  transfers between devices with their start and end apart: 13 -> 12, of which waited for: 1 -> 0; matrix products, arithmetic and copies ran while one was open for 10% -> 14% of each run, Pallas kernels for 15% -> 8%
where the time goes in v2:
time: 364 us; the launch traced here: 357 us
  Pallas kernels  266 us (73%)
  matrix products  35 us (10%)
  other arithmetic  27.7 us (8%)
  local copies, waits for them, and re-layouts  22.5 us (6%)
    pallas_call x1, Pallas kernels, dp_sum(): pl.pallas_call(functools.partial(dp_sum_kernel, count, plan), in_specs=[v...  138 us
    pallas_call x5, Pallas kernels, call(): pl.pallas_call(kernel, grid=(grid,), in_specs=[pl.BlockSpec(b, m) for _,...  128 us
    dot_general x12, matrix products, tn(): lax.dot_general(a, b, (((0,), (0,)), ((), ())), preferred_element_type=F32)  35 us
    concatenate x1, other arithmetic, local(): wide = jnp.concatenate(qkv_grad + [out_grad], axis=1)  7.62 us
  transfers between devices with their start and end apart: 12, of which 0 were waited for; matrix products, arithmetic and copies ran while one was open for 14% of the time, Pallas kernels for 8%

profile of v2, /device:TPU:0, one launch (start us, length us, event | category | flops | bytes accessed | tf_op | source)
XLA Modules:
  0.0 356.7 jit_solution(8962525619006146330)
XLA Ops:
  0.7 0.7 reshape.110
  1.4 0.7 constant_dynamic-update-slice_fusion.12
  2.1 0.7 constant_dynamic-update-slice_fusion.9
  2.8 0.7 constant_dynamic-update-slice_fusion.6
  3.5 0.7 constant_dynamic-update-slice_fusion.3
  4.2 0.7 constant_dynamic-update-slice_fusion
  4.9 0.5 collective-permute-start.1
  6.4 0.7 fusion.37
  7.1 0.9 compare_reduce_fusion
  8.6 1.9 fusion.16
  10.7 1.9 pad_maximum_fusion.2
  12.6 0.6 constant_dynamic-slice_fusion.srow_ref
  13.2 0.6 broadcast_in_dim.47.gain_ref
  13.7 0.6 broadcast_in_dim.48.bias_ref
  14.3 1.0 copy.52.scol_ref
  15.3 0.6 broadcast_in_dim.52.ob_ref
  15.9 0.6 broadcast_in_dim.53.ng_ref
  16.5 0.6 broadcast_in_dim.54.nb_ref
  17.1 0.6 broadcast_in_dim.58.db_ref
  17.7 0.6 broadcast_in_dim.50.sg_ref
  18.3 0.6 broadcast_in_dim.51.sb_ref
  18.9 0.6 pad_maximum_fusion.4.qb_ref
  19.5 0.6 pad_maximum_fusion.7
  20.1 0.6 pad_maximum_fusion.5
  20.7 9.3 %project.1 = (bf16[1024,768]{1,0:T(8,128)(2,1)}, bf16[1024,768]{1,0:T(8,128)(2,1)}, bf16[1024,768]{1,0:T(8,128)(2,1)}, bf16[1024,768]{1,0:T(8,128)(2,1)}) custom-call(bf16[1024,768]{1,0:T(8,128)(2,1)} %bitcast.62, f32[1,768]{1,0:T(1,128)} %broadcast_in_dim.47.gain_ref, f32[1,768]{1,0:T(1,128)} %broadcast_in_dim.48.bias_ref, bf16[3,768,384]{2,1,0:T(8,128)(2,1)} %own_ref.3, ...), custom_call_target="tpu_custom_call" | custom-call | flops 3623878656 | bytes 12467200 | tf_op jit(solution)/shard_map/project/pallas_call | solution.py:327
  30.1 20.4 %attend.1 = (f32[1024,768]{1,0:T(8,128)}, f32[6,8,1024]{2,1,0:T(8,128)}) custom-call(bf16[1024,768]{1,0:T(8,128)(2,1)} %get-tuple-element.54.q_ref, bf16[1024,768]{1,0:T(8,128)(2,1)} %get-tuple-element.55.k_ref, bf16[1024,768]{1,0:T(8,128)(2,1)} %get-tuple-element.56.v_ref, s32[1024,1]{1,0:T(8,128)} %copy.52.scol_ref, ...), custom_call_target="tpu_custom_call" | custom-call | flops 7247757312 | bytes 8069120 | tf_op jit(solution)/shard_map/attend/pallas_call | solution.py:327
  50.5 0.8 copy-done.28
  51.3 0.8 copy-done.25
  52.1 60.5 %middle.1 = (bf16[1024,768]{1,0:T(8,128)(2,1)}, f32[1024,768]{1,0:T(8,128)}, bf16[1024,768]{1,0:T(8,128)(2,1)}, bf16[1024,768]{1,0:T(8,128)(2,1)}, bf16[1024,768...) custom-call(bf16[1024,768]{1,0:T(8,128)(2,1)} %bitcast.63, ...), custom_call_target="tpu_custom_call" | custom-call | flops 21743271936 | bytes 40611840 | tf_op jit(solution)/shard_map/middle/pallas_call | solution.py:327
  112.6 26.3 %attend_back.1 = (bf16[1024,768]{1,0:T(8,128)(2,1)}, bf16[1024,768]{1,0:T(8,128)(2,1)}, bf16[1024,768]{1,0:T(8,128)(2,1)}, f32[1,768]{1,0:T(1,128)}, f32[1,768]{1,0:T(1,128)}, /*index=5*/f32[1,768]{1,0:T(1,128)}) custom-call(bf16[1024,768]{1,0:T(8,128)(2,1)} %get-tuple-element.54.q_ref, bf16[1024,768]{1,0:T(8,128)(2,1)} %get-tuple-element.55.k_ref, ...), custom_call_target="tpu_custom_call" | custom-call | flops 18119393280 | bytes 12272640 | tf_op jit(solution)/shard_map/attend_back/pallas_call | solution.py:327
  138.9 0.7 slice_reduce_fusion.11
  139.7 0.7 slice_reduce_fusion.10
  140.4 0.7 slice_reduce_fusion.9
  141.3 2.1 convolution_convert_fusion.5
  143.5 0.9 convolution_convert_fusion.4
  144.3 0.5 copy-done.29
  144.9 0.8 convolution_convert_fusion.3
  145.8 11.5 %finish.1 = (f32[1024,768]{1,0:T(8,128)}, f32[1,768]{1,0:T(1,128)}, f32[1,768]{1,0:T(1,128)}) custom-call(bf16[1024,768]{1,0:T(8,128)(2,1)} %bitcast.64, f32[1024,768]{1,0:T(8,128)} %get-tuple-element.59.dmid_ref, bf16[1024,768]{1,0:T(8,128)(2,1)} %get-tuple-element.62.dq_ref, bf16[1024,768]{1,0:T(8,128)(2,1)} %get-tuple-element.63.dk_ref, ...), custom_call_target="tpu_custom_call" | custom-call | flops 3623878656 | bytes 16131072 | tf_op jit(solution)/shard_map/finish/pallas_call | solution.py:327
  157.2 0.7 reduce.10
  157.9 0.7 reduce.11
  159.2 0.5 collective-permute-start.7
  160.2 6.5 %convolution_convert_fusion = bf16[768,1536]{1,0:T(8,128)(2,1)} fusion(bf16[1024,768]{1,0:T(8,128)(2,1)} %get-tuple-element.67, bf16[1024,3072]{1,0:T(8,128)(2,1)} %get-tuple-element.68), kind=kOutput, calls=%fused_computation.3 | convolution fusion | flops 2417098752 | bytes 7077888 | tf_op jit(solution)/shard_map/dot_general | solution.py:29
  166.8 6.1 %convolution_convert_fusion.1 = bf16[1536,768]{1,0:T(8,128)(2,1)} fusion(bf16[1024,3072]{1,0:T(8,128)(2,1)} %get-tuple-element.66, bf16[1,1024,768]{2,1,0:T(8,128)(2,1)S(1)} %copy-done.26), kind=kOutput, calls=%fused_computation.4 | convolution fusion | flops 2417098752 | bytes 7077888 | tf_op jit(solution)/shard_map/dot_general | solution.py:29
  172.9 1.0 convolution_convert_fusion.2
  174.5 0.6 concatenate.65
  175.2 0.9 fusion.4
  176.1 1.0 fusion.7
  177.5 0.9 fusion.5
  178.7 0.9 fusion.6
  179.5 7.6 %maximum_maximum_fusion = bf16[768,1536]{0,1:T(8,128)(2,1)S(1)} fusion(bf16[384,384]{0,1:T(8,128)(2,1)S(1)} %get-tuple-element.112, bf16[384,384]{0,1:T(8,128)(2,1)S(1)} %get-tuple-element.111, bf16[768,384]{0,1:T(8,128)(2,1)S(1)} %fusion.6, bf16[768,384]{0,1:T(8,128)(2,1)S(1)} %fusion.5, bf16[768,384]{0,1:T(8,128)(2,1)S(1)} %fusion.4), kind=kLoop, calls=%fused_computation.9 | loop fusion | flops 11796480 | bytes 4718592 | tf_op jit(solution)/shard_map/concatenate | solution.py:613
  187.2 2.4 copy.59
  189.6 7.2 %add_convert_fusion = bf16[768,1536]{1,0:T(8,128)(2,1)} fusion(bf16[768,1536]{1,0:T(8,128)(2,1)} %collective-permute-done.6, bf16[1024,768]{1,0:T(8,128)(2,1)} %get-tuple-element.67, bf16[1024,3072]{1,0:T(8,128)(2,1)} %get-tuple-element.68), kind=kOutput, calls=%fused_computation | convolution fusion | flops 2419458048 | bytes 9437184 | tf_op jit(solution)/shard_map/dot_general | solution.py:29
  196.9 6.7 %add_convert_fusion.1 = bf16[1536,768]{1,0:T(8,128)(2,1)} fusion(bf16[1536,768]{1,0:T(8,128)(2,1)} %collective-permute-done.5, bf16[1024,3072]{1,0:T(8,128)(2,1)} %get-tuple-element.66, bf16[1,1024,768]{2,1,0:T(8,128)(2,1)S(1)} %copy-done.27), kind=kOutput, calls=%fused_computation.1 | convolution fusion | flops 2419458048 | bytes 9437184 | tf_op jit(solution)/shard_map/dot_general | solution.py:29
  203.6 138.2 %dp_sum.1 = (bf16[16,96,768]{2,1,0:T(8,128)(2,1)}, bf16[16,48,1536]{2,1,0:T(8,128)(2,1)}, bf16[16,48,1536]{2,1,0:T(8,128)(2,1)}, bf16[16,16,128]{2,1,0:T(8,128)(2,1)}) custom-call(bf16[16,96,768]{2,1,0:T(8,128)(2,1)} %bitcast.54, bf16[16,48,1536]{2,1,0:T(8,128)(2,1)} %bitcast.53, bf16[16,48,1536]{2,1,0:T(8,128)(2,1)} %bitcast.52, bf16[16,16,128]{2,1,0:T(8,128)(2,1)} %bitcast.55), custom_call_target="tpu_custom_call" | custom-call | tf_op jit(solution)/shard_map/dp_sum/pallas_call | solution.py:458
  341.7 2.3 bitcast_convert_fusion.2
  344.4 0.6 copy-done.2
  345.0 0.6 fusion.24
  345.6 0.6 fusion.22
  346.2 0.6 fusion.23
  346.8 2.7 bitcast_convert_fusion
  349.5 3.0 bitcast_convert_fusion.1
  352.5 1.1 pad_maximum_fusion.1
  353.6 0.6 pad_maximum_fusion.8
  354.2 2.0 pad_maximum_fusion
  (146 shorter events, 4.5 us)
Async XLA Ops:
  4.9 12.8 %collective-permute-start.1 = (f32[6528]{0:T(1024)S(1)}, f32[6528]{0:T(1024)S(1)}, u32[]{:S(2)}, u32[]{:S(2)}) collective-permute-start(f32[6528]{0:T(1024)S(1)} %constant_dynamic-update-slice_fusion), channel_id=1, source_target_pairs={{0,1},{1,0},{2,3},{3,2},{4,5},{5,4},{6,7},{7,6},{8,9},{9,8},{10,11... | collective-permute-start | bytes 78344 | tf_op jit(solution)/shard_map/ppermute | solution.py:487
  5.4 15.4 %collective-permute-start = (bf16[3,768,384]{2,1,0:T(8,128)(2,1)}, bf16[3,768,384]{2,1,0:T(8,128)(2,1)}, u32[]{:S(2)}, u32[]{:S(2)}) collective-permute-start(bf16[3,768,384]{2,1,0:T(8,128)(2,1)} %own_ref.3), channel_id=1, source_target_pairs={{0,1},{1,0},{2,3},{3,2},{4,5},{5,4},{6,7},{7,6},{8,9},{9,8},{10,11... | collective-permute-start | bytes 5308424 | tf_op jit(solution)/shard_map/ppermute | solution.py:487
  5.4 45.1 %collective-permute-start.3 = (bf16[768,1536]{1,0:T(8,128)(2,1)}, bf16[768,1536]{1,0:T(8,128)(2,1)S(1)}, u32[]{:S(2)}, u32[]{:S(2)}) collective-permute-start(bf16[768,1536]{1,0:T(8,128)(2,1)} %wu0_ref.1), channel_id=1, source_target_pairs={{0,1},{1,0},{2,3},{3,2},{4,5},{5,4},{6,7},{7,6},{8,9},{9,8},{10,11... | collective-permute-start | bytes 7077896 | tf_op jit(solution)/shard_map/ppermute | solution.py:487
  5.9 44.6 %collective-permute-start.4 = (bf16[1536,768]{1,0:T(8,128)(2,1)}, bf16[1536,768]{1,0:T(8,128)(2,1)}, u32[]{:S(2)}, u32[]{:S(2)}) collective-permute-start(bf16[1536,768]{1,0:T(8,128)(2,1)} %wd0_ref.1), channel_id=1, source_target_pairs={{0,1},{1,0},{2,3},{3,2},{4,5},{5,4},{6,7},{7,6},{8,9},{9,8},{10,11... | collective-permute-start | bytes 7077896 | tf_op jit(solution)/shard_map/ppermute | solution.py:487
  5.9 44.6 %collective-permute-start.2 = (bf16[384,768]{1,0:T(8,128)(2,1)}, bf16[384,768]{1,0:T(8,128)(2,1)S(1)}, u32[]{:S(2)}, u32[]{:S(2)}) collective-permute-start(bf16[384,768]{1,0:T(8,128)(2,1)} %wo0_ref.1), channel_id=1, source_target_pairs={{0,1},{1,0},{2,3},{3,2},{4,5},{5,4},{6,7},{7,6},{8,9},{9,8},{10,11... | collective-permute-start | bytes 1769480 | tf_op jit(solution)/shard_map/ppermute | solution.py:487
  10.5 2.0 copy-start.6
  10.5 2.6 copy-start.13
  10.6 3.2 copy-start.14
  10.6 4.8 %copy-start.15 = (f32[768]{0:T(1024)S(1)}, f32[768]{0:T(1024)}, u32[]{:S(2)}) copy-start(f32[768]{0:T(1024)} %param.29) | copy-start | bytes 9220
  10.6 5.3 %copy-start.16 = (f32[768]{0:T(1024)S(1)}, f32[768]{0:T(1024)}, u32[]{:S(2)}) copy-start(f32[768]{0:T(1024)} %param.30) | copy-start | bytes 9220
  10.6 5.9 %copy-start.17 = (f32[768]{0:T(1024)S(1)}, f32[768]{0:T(1024)}, u32[]{:S(2)}) copy-start(f32[768]{0:T(1024)} %param.31) | copy-start | bytes 9220
  10.6 6.5 %copy-start.18 = (f32[768]{0:T(1024)S(1)}, f32[768]{0:T(1024)}, u32[]{:S(2)}) copy-start(f32[768]{0:T(1024)} %param.37) | copy-start | bytes 9220
  10.6 7.1 %copy-start.11 = (f32[384]{0:T(512)S(1)}, f32[384]{0:T(512)}, u32[]{:S(2)}) copy-start(f32[384]{0:T(512)} %param.26) | copy-start | bytes 4612
  10.6 7.1 %copy-start.12 = (f32[384]{0:T(512)S(1)}, f32[384]{0:T(512)}, u32[]{:S(2)}) copy-start(f32[384]{0:T(512)} %param.27) | copy-start | bytes 4612
  10.6 8.3 %copy-start.7 = (f32[3,384]{1,0:T(4,128)S(1)}, f32[3,384]{1,0:T(4,128)}, u32[]{:S(2)}) copy-start(f32[3,384]{1,0:T(4,128)} %param.25) | copy-start | bytes 13828
  10.6 8.9 %copy-start.3 = (f32[1536]{0:T(1024)S(1)}, f32[1536]{0:T(1024)}, u32[]{:S(2)}) copy-start(f32[1536]{0:T(1024)} %param.35) | copy-start | bytes 18436
  10.7 9.5 %copy-start.4 = (f32[1536]{0:T(1024)S(1)}, f32[1536]{0:T(1024)}, u32[]{:S(2)}) copy-start(f32[1536]{0:T(1024)} %param.33) | copy-start | bytes 18436
  10.7 9.4 %copy-start.5 = (f32[1536]{0:T(1024)S(1)}, f32[1536]{0:T(1024)}, u32[]{:S(2)}) copy-start(f32[1536]{0:T(1024)} %param.34) | copy-start | bytes 18436
  50.5 0.8 copy-start.28
  50.5 1.6 copy-start.25
  112.6 28.5 %copy-start.20 = (f32[1,768]{1,0:T(1,128)S(1)}, f32[1,768]{1,0:T(1,128)}, u32[]{:S(2)}) copy-start(f32[1,768]{1,0:T(1,128)} %get-tuple-element.75) | copy-start | bytes 9220
  112.6 28.6 %copy-start.19 = (f32[1,768]{1,0:T(1,128)S(1)}, f32[1,768]{1,0:T(1,128)}, u32[]{:S(2)}) copy-start(f32[1,768]{1,0:T(1,128)} %get-tuple-element.76) | copy-start | bytes 9220
  112.6 28.6 %copy-start.10 = (f32[1,3072]{1,0:T(1,128)S(1)}, f32[1,3072]{1,0:T(1,128)}, u32[]{:S(2)}) copy-start(f32[1,3072]{1,0:T(1,128)} %get-tuple-element.77) | copy-start | bytes 36868
  112.6 28.6 %copy-start.9 = (f32[1,3072]{1,0:T(1,128)S(1)}, f32[1,3072]{1,0:T(1,128)}, u32[]{:S(2)}) copy-start(f32[1,3072]{1,0:T(1,128)} %get-tuple-element.78) | copy-start | bytes 36868
  112.6 28.7 %copy-start.8 = (f32[1,3072]{1,0:T(1,128)S(1)}, f32[1,3072]{1,0:T(1,128)}, u32[]{:S(2)}) copy-start(f32[1,3072]{1,0:T(1,128)} %get-tuple-element.79) | copy-start | bytes 36868
  112.6 28.7 %copy-start.36 = (bf16[1024,768]{1,0:T(8,128)(2,1)S(1)}, bf16[1024,768]{1,0:T(8,128)(2,1)}, u32[]{:S(2)}) copy-start(bf16[1024,768]{1,0:T(8,128)(2,1)} %get-tuple-element.69) | copy-start | bytes 4718596
  141.3 2.1 copy-start.31
  143.5 1.4 copy-start.29
  145.7 12.9 %copy-start.24 = (f32[1,768]{1,0:T(1,128)S(1)}, f32[1,768]{1,0:T(1,128)}, u32[]{:S(2)}) copy-start(f32[1,768]{1,0:T(1,128)} %get-tuple-element.82) | copy-start | bytes 9220
  145.7 13.0 %copy-start.23 = (f32[1,768]{1,0:T(1,128)S(1)}, f32[1,768]{1,0:T(1,128)}, u32[]{:S(2)}) copy-start(f32[1,768]{1,0:T(1,128)} %get-tuple-element.83) | copy-start | bytes 9220
  145.7 13.0 %copy-start.22 = (f32[1,768]{1,0:T(1,128)S(1)}, f32[1,768]{1,0:T(1,128)}, u32[]{:S(2)}) copy-start(f32[1,768]{1,0:T(1,128)} %get-tuple-element.84) | copy-start | bytes 9220
  145.7 13.0 %copy-start.21 = (f32[1,768]{1,0:T(1,128)S(1)}, f32[1,768]{1,0:T(1,128)}, u32[]{:S(2)}) copy-start(f32[1,768]{1,0:T(1,128)} %get-tuple-element.85) | copy-start | bytes 9220
  159.1 14.9 %collective-permute-start.11 = (f32[11136]{0:T(1024)S(1)}, f32[11136]{0:T(1024)S(1)}, u32[]{:S(2)}, u32[]{:S(2)}) collective-permute-start(f32[11136]{0:T(1024)S(1)} %get-tuple-element.135), channel_id=1, source_target_pairs={{0,1},{1,0},{2,3},{3,2},{4,5},{5,4},{6,7},{7,6},{8,9},{9,8},{10,11... | collective-permute-start | bytes 133640 | tf_op jit(solution)/shard_map/ppermute | solution.py:487
  159.2 15.9 %collective-permute-start.7 = (bf16[768,384]{0,1:T(8,128)(2,1)S(1)}, bf16[768,384]{0,1:T(8,128)(2,1)S(1)}, u32[]{:S(2)}, u32[]{:S(2)}) collective-permute-start(bf16[768,384]{0,1:T(8,128)(2,1)S(1)} %convolution_convert_fusion.5), channel_id=1, source_target_pairs={{0,1},{1,0},{2,3},{3,2},{4,5},{5,4},{6,7},{7,6},{8,9},{9,8},{10,11... | collective-permute-start | bytes 1769480 | tf_op jit(solution)/shard_map/ppermute | solution.py:487
  159.7 17.5 %collective-permute-start.8 = (bf16[768,384]{0,1:T(8,128)(2,1)S(1)}, bf16[768,384]{0,1:T(8,128)(2,1)S(1)}, u32[]{:S(2)}, u32[]{:S(2)}) collective-permute-start(bf16[768,384]{0,1:T(8,128)(2,1)S(1)} %convolution_convert_fusion.4), channel_id=1, source_target_pairs={{0,1},{1,0},{2,3},{3,2},{4,5},{5,4},{6,7},{7,6},{8,9},{9,8},{10,11... | collective-permute-start | bytes 1769480 | tf_op jit(solution)/shard_map/ppermute | solution.py:487
  159.7 18.6 %collective-permute-start.9 = (bf16[768,384]{0,1:T(8,128)(2,1)S(1)}, bf16[768,384]{0,1:T(8,128)(2,1)S(1)}, u32[]{:S(2)}, u32[]{:S(2)}) collective-permute-start(bf16[768,384]{0,1:T(8,128)(2,1)S(1)} %convolution_convert_fusion.3), channel_id=1, source_target_pairs={{0,1},{1,0},{2,3},{3,2},{4,5},{5,4},{6,7},{7,6},{8,9},{9,8},{10,11... | collective-permute-start | bytes 1769480 | tf_op jit(solution)/shard_map/ppermute | solution.py:487
  160.2 6.6 %copy-start.26 = (bf16[1,1024,768]{2,1,0:T(8,128)(2,1)S(1)}, bf16[1,1024,768]{2,1,0:T(8,128)(2,1)}, u32[]{:S(2)}) copy-start(bf16[1,1024,768]{2,1,0:T(8,128)(2,1)} %param.21) | copy-start | bytes 4718596
  166.7 22.9 %collective-permute-start.6 = (bf16[768,1536]{1,0:T(8,128)(2,1)}, bf16[768,1536]{1,0:T(8,128)(2,1)}, u32[]{:S(2)}, u32[]{:S(2)}) collective-permute-start(bf16[768,1536]{1,0:T(8,128)(2,1)} %convolution_convert_fusion), channel_id=1, source_target_pairs={{0,1},{1,0},{2,3},{3,2},{4,5},{5,4},{6,7},{7,6},{8,9},{9,8},{10,11... | collective-permute-start | bytes 7077896 | tf_op jit(solution)/shard_map/ppermute | solution.py:487
  166.8 6.1 %copy-start.34 = (bf16[1024,768]{1,0:T(8,128)(2,1)S(1)}, bf16[1024,768]{1,0:T(8,128)(2,1)}, u32[]{:S(2)}) copy-start(bf16[1024,768]{1,0:T(8,128)(2,1)} %get-tuple-element.71) | copy-start | bytes 4718596
  166.8 6.1 %copy-start.35 = (bf16[1024,768]{1,0:T(8,128)(2,1)S(1)}, bf16[1024,768]{1,0:T(8,128)(2,1)}, u32[]{:S(2)}) copy-start(bf16[1024,768]{1,0:T(8,128)(2,1)} %get-tuple-element.70) | copy-start | bytes 4718596
  172.9 2.3 copy-start.33
  174.0 2.1 collective-permute-start.10
  175.1 21.8 %collective-permute-start.5 = (bf16[1536,768]{1,0:T(8,128)(2,1)}, bf16[1536,768]{1,0:T(8,128)(2,1)}, u32[]{:S(2)}, u32[]{:S(2)}) collective-permute-start(bf16[1536,768]{1,0:T(8,128)(2,1)} %convolution_convert_fusion.1), channel_id=1, source_target_pairs={{0,1},{1,0},{2,3},{3,2},{4,5},{5,4},{6,7},{7,6},{8,9},{9,8},{10,11... | collective-permute-start | bytes 7077896 | tf_op jit(solution)/shard_map/ppermute | solution.py:487
  176.0 1.4 copy-start.32
  177.2 1.5 copy-start.30
  189.6 7.3 %copy-start.27 = (bf16[1,1024,768]{2,1,0:T(8,128)(2,1)S(1)}, bf16[1,1024,768]{2,1,0:T(8,128)(2,1)}, u32[]{:S(2)}) copy-start(bf16[1,1024,768]{2,1,0:T(8,128)(2,1)} %param.21) | copy-start | bytes 4718596
  344.1 0.8 copy-start.2
  344.1 2.7 copy-start.1
  346.8 2.7 copy-start
